TPU v7x, 256 devices: a whole 4x4x8 slice. The times are simulated.
256 devices in a mesh: gx: 32 (over z, y), gy: 4 (over x_lo, core), gz: 2 (over x_hi).
Axes of the slice: x: 4 (x_hi: 2, x_lo: 2; x = x_hi * 2 + x_lo), y: 4, z: 8, core: 2. Of those that a mesh axis runs over, the one named last changes fastest.
Arguments:
- weights: float32 [3, 128, 128, 512], P(None, 'gx', 'gz', 'gy'), may hold values from 0.2 to 2
- abscissas: float32 [3, 128, 128, 512], P(None, 'gx', 'gz', 'gy'), may hold values from -4 to 4, as said below
Outputs:
- moments_end: float32 [6, 128, 128, 512], P(None, 'gx', 'gz', 'gy')
Inputs may be any that keep to these rules, and one draw needn't show every extreme that they name: In every cell the three abscissas increase with the node index, consecutive ones at least 0.25 apart.
All inputs are finite; a program needn't handle non-finite values. Where the computation divides by a largest or mean magnitude, that divisor is 1e-20 or more.
Results may differ from a plain program's by a relative error of at most 0.0003.
Values sent between devices are 32-bit elements; how exact they have to be, the bound alone decides.
No kernel may reach another device: no remote copies, remote signals or barrier semaphores. Data moves between devices by JAX's collectives and lax.ppermute only.
A program may use at most 128 MiB of HBM per device.

v0:
```python
import functools
import math

import jax
import jax.numpy as jnp
from jax import lax
from jax.sharding import Mesh
from jax.sharding import PartitionSpec as P

GX_GY_GZ = ("gx_0", "gx_1", "gy_0", "gy_1", "gz")
GX = ("gx_0", "gx_1")
GY = ("gy_0", "gy_1")


COURANT = 0.4
SPEED_TOTAL = 1.72
AXIS_SPEEDS = ((1, 0.6), (2, 0.64), (3, 0.48))


def by_axis(value, axes):
    return functools.reduce(lax.pmax, axes, value)


def extended(value, sides, width):
    edges = {}
    for axis, dim in sides:
        count, length = (lax.axis_size(axis), value.shape[dim])
        up = [(i, (i + 1) % count) for i in range(count)]
        last = lax.slice_in_dim(value, length - width, length, axis=dim)
        initial = lax.slice_in_dim(value, 0, width, axis=dim)
        edges[dim] = (
            lax.ppermute(last, axis, up),
            lax.ppermute(initial, axis, [(b, a) for a, b in up]),
        )
    done = []
    for _, dim in sides:
        low, high = edges[dim]
        around = [(width, width) if d in done else (0, 0) for d in range(value.ndim)]
        value = jnp.concatenate([jnp.pad(low, around), value, jnp.pad(high, around)], axis=dim)
        done.append(dim)
    return value


def minmod(first, second):
    return jnp.where(
        first * second > 0.0, jnp.sign(first) * jnp.minimum(jnp.abs(first), jnp.abs(second)), 0.0
    )


def cut_along(array, lower, upper, array_axis):
    return lax.slice_in_dim(array, lower, upper, axis=array_axis)


def moments_of(node_weights, node_speeds):
    result = []
    power = node_weights
    for order in range(6):
        result.append(jnp.sum(power, axis=0))
        power = power * node_speeds
    return jnp.stack(result)


def face_divergence(node_weights, node_speeds):
    total = None
    for array_axis, component in AXIS_SPEEDS:
        window = [slice(None), slice(2, -2), slice(2, -2), slice(2, -2)]
        window[array_axis] = slice(None)
        line_w = node_weights[tuple(window)]
        line_u = node_speeds[tuple(window)]
        length = line_w.shape[array_axis]
        jumps = cut_along(line_w, 1, length, array_axis) - cut_along(
            line_w, 0, length - 1, array_axis
        )
        slopes = minmod(
            cut_along(jumps, 0, length - 2, array_axis), cut_along(jumps, 1, length - 1, array_axis)
        )
        left_w = cut_along(line_w, 1, length - 2, array_axis) + 0.5 * cut_along(
            slopes, 0, length - 3, array_axis
        )
        right_w = cut_along(line_w, 2, length - 1, array_axis) - 0.5 * cut_along(
            slopes, 1, length - 2, array_axis
        )
        left_u = cut_along(line_u, 1, length - 2, array_axis)
        right_u = cut_along(line_u, 2, length - 1, array_axis)
        left_term = component * left_w * jnp.maximum(left_u, 0.0)
        right_term = component * right_w * jnp.minimum(right_u, 0.0)
        fluxes = []
        for order in range(6):
            fluxes.append(jnp.sum(left_term + right_term, axis=0))
            left_term = left_term * left_u
            right_term = right_term * right_u
        flux = jnp.stack(fluxes)
        faces = length - 3
        diverge = cut_along(flux, 1, faces, array_axis) - cut_along(flux, 0, faces - 1, array_axis)
        total = diverge if total is None else total + diverge
    return total


def invert(moments):
    mom = [moments[index] for index in range(6)]
    mean_one = mom[1] / mom[0]
    first_row = [None] + [mom[level + 1] - mean_one * mom[level] for level in range(1, 5)]
    mean_two = first_row[2] / first_row[1] - mean_one
    spread_one = first_row[1] / mom[0]
    second_two = first_row[3] - mean_two * first_row[2] - spread_one * mom[2]
    second_three = first_row[4] - mean_two * first_row[3] - spread_one * mom[3]
    mean_three = second_three / second_two - first_row[2] / first_row[1]
    spread_two = second_two / first_row[1]
    centre = (mean_one + mean_two + mean_three) / 3.0
    dev_one = mean_one - centre
    dev_two = mean_two - centre
    dev_three = mean_three - centre
    radius = jnp.sqrt(
        (
            dev_one * dev_one
            + dev_two * dev_two
            + dev_three * dev_three
            + 2.0 * spread_one
            + 2.0 * spread_two
        )
        / 6.0
    )
    determinant = dev_one * dev_two * dev_three - dev_one * spread_two - dev_three * spread_one
    ratio = determinant / (2.0 * radius * radius * radius)
    angle = jnp.arccos(ratio) / 3.0
    highest = centre + 2.0 * radius * jnp.cos(angle)
    lowest = centre + 2.0 * radius * jnp.cos(angle + 2.0 * math.pi / 3.0)
    middle = 3.0 * centre - highest - lowest
    root_one = jnp.sqrt(spread_one)
    root_two = jnp.sqrt(spread_two)
    speeds = []
    masses = []
    for value in (lowest, middle, highest):
        first_comp = (value - mean_one) / root_one
        second_comp = ((value - mean_two) * first_comp - root_one) / root_two
        masses.append(mom[0] / (1.0 + first_comp * first_comp + second_comp * second_comp))
        speeds.append(value)
    return (jnp.stack(masses), jnp.stack(speeds))


def local(weights, abscissas):
    moments_start = moments_of(weights, abscissas)
    fastest = by_axis(jnp.max(jnp.abs(abscissas)), GX_GY_GZ)
    step_one = COURANT / (SPEED_TOTAL * fastest)
    entry_w, entry_u = (
        extended(weights, ((GX, 1), (GY, 3), ("gz", 2)), 2),
        extended(abscissas, ((GX, 1), (GY, 3), ("gz", 2)), 2),
    )
    moments_mid = moments_start - step_one * face_divergence(entry_w, entry_u)
    mid_weights, inner_speeds = invert(moments_mid)
    padded_w, padded_u = (
        extended(mid_weights, ((GX, 1), (GY, 3), ("gz", 2)), 2),
        extended(inner_speeds, ((GX, 1), (GY, 3), ("gz", 2)), 2),
    )
    fastest_mid = by_axis(jnp.max(jnp.abs(inner_speeds)), GX_GY_GZ)
    step_two = COURANT / (SPEED_TOTAL * fastest_mid)
    change = face_divergence(padded_w, padded_u)
    return 0.5 * moments_start + 0.5 * (moments_mid - step_two * change)


def solution(mesh):
    split = Mesh(
        mesh.devices.reshape(8, 4, 2, 2, mesh.shape["gz"]), ("gx_0", "gx_1", "gy_0", "gy_1", "gz")
    )
    in_specs = (P(None, GX, "gz", GY), P(None, GX, "gz", GY))
    out_specs = P(None, GX, "gz", GY)
    return jax.shard_map(local, mesh=split, in_specs=in_specs, out_specs=out_specs, check_vma=False)
```

profile of v0, /device:TPU:1, one launch (start us, length us, event | category | flops | bytes accessed | tf_op | source)
XLA Modules:
  0.0 198.3 jit_solution(8355528034073102826)
XLA Ops:
  6.5 2.4 %collective-permute-start.5 = (f32[3,4,64,2]{3,2,1,0:T(8,128)S(1)}, f32[3,4,64,2]{3,2,1,0:T(8,128)S(1)}, u32[]{:S(2)}, u32[]{:S(2)}) collective-permute-start(f32[3,4,64,2]{3,2,1,0:T(8,128)S(1)} %get-tuple-element.107), channel_id=1, source_target_pairs={{0,2},{2,4},{4,6},{6,0},{1,3},{3,5},{5,7},{7,1},{8,10},{10,12},{12... | collective-permute-start | bytes 18440 | tf_op jit(solution)/shard_map/ppermute | solution.py:32
  10.9 6.1 %collective-permute-done.5 = f32[3,4,64,2]{3,2,1,0:T(8,128)S(1)} collective-permute-done((f32[3,4,64,2]{3,2,1,0:T(8,128)S(1)}, f32[3,4,64,2]{3,2,1,0:T(8,128)S(1)}, u32[]{:S(2)}, u32[]{:S(2)}) %collective-permute-start.5) | collective-permute-done | bytes 6176 | tf_op jit(solution)/shard_map/ppermute | solution.py:32
  20.6 2.5 %collective-permute-start.7 = (f32[3,4,2,128]{3,2,1,0:T(2,128)S(1)}, f32[3,4,2,128]{3,2,1,0:T(2,128)S(1)}, u32[]{:S(2)}, u32[]{:S(2)}) collective-permute-start(f32[3,4,2,128]{3,2,1,0:T(2,128)S(1)} %get-tuple-element.100), channel_id=1, source_target_pairs={{1,0},{0,1},{3,2},{2,3},{5,4},{4,5},{7,6},{6,7},{9,8},{8,9},{11,10... | collective-permute-start | bytes 36872 | tf_op jit(solution)/shard_map/ppermute | solution.py:33
  25.4 4.9 %collective-permute-done.10 = f32[3,4,64,2]{3,2,1,0:T(8,128)S(1)} collective-permute-done((f32[3,4,64,2]{3,2,1,0:T(8,128)S(1)}, f32[3,4,64,2]{3,2,1,0:T(8,128)S(1)}, u32[]{:S(2)}, u32[]{:S(2)}) %collective-permute-start.10) | collective-permute-done | bytes 6176 | tf_op jit(solution)/shard_map/ppermute | solution.py:33
  30.3 4.9 %collective-permute-start.1 = (f32[3,2,64,128]{3,2,1,0:T(8,128)S(1)}, f32[3,2,64,128]{3,2,1,0:T(8,128)S(1)}, u32[]{:S(2)}, u32[]{:S(2)}) collective-permute-start(f32[3,2,64,128]{3,2,1,0:T(8,128)S(1)} %get-tuple-element.109), channel_id=1, source_target_pairs={{8,0},{16,8},{24,16},{32,24},{40,32},{48,40},{56,48},{64,56},{72,6... | collective-permute-start | bytes 589832 | tf_op jit(solution)/shard_map/ppermute | solution.py:33
  38.6 2.3 %collective-permute-start.11 = (f32[3,4,2,128]{3,2,1,0:T(2,128)}, f32[3,4,2,128]{3,2,1,0:T(2,128)S(1)}, u32[]{:S(2)}, u32[]{:S(2)}) collective-permute-start(f32[3,4,2,128]{3,2,1,0:T(2,128)} %get-tuple-element.98), channel_id=1, source_target_pairs={{1,0},{0,1},{3,2},{2,3},{5,4},{4,5},{7,6},{6,7},{9,8},{8,9},{11,10... | collective-permute-start | bytes 36872 | tf_op jit(solution)/shard_map/ppermute | solution.py:33
  49.6 12.9 %pmax.70 = f32[]{:T(128)} all-reduce(f32[]{:T(128)} %get-tuple-element.44), channel_id=1, replica_groups=mesh['gx_0'=8,'gx_1'=4,'gy_0'=2,'gy_1'=2,'gz'=2] {'gx_0'}, use_global_device_ids=true, to_apply=%region_7.0 | all-reduce | flops 1 | bytes 8 | tf_op jit(solution)/shard_map/pmax | solution.py:21
  70.0 7.9 %pmax.71 = f32[]{:T(128)} all-reduce(f32[]{:T(128)} %pmax.70), channel_id=1, replica_groups=mesh['gx_0'=8,'gx_1'=4,'gy_0'=2,'gy_1'=2,'gz'=2] {'gx_1'}, use_global_device_ids=true, to_apply=%region_8.0 | all-reduce | flops 1 | bytes 8 | tf_op jit(solution)/shard_map/pmax | solution.py:21
  77.9 2.2 %add_reduce_fusion.22 = (f32[5,64,128]{2,1,0:T(8,128)}, f32[3,5,64,128]{3,2,1,0:T(8,128)S(1)}, f32[3,5,64,128]{3,2,1,0:T(8,128)S(1)}) fusion(f32[3,4,64,128]{3,2,1,0:T(8,128)S(1)} %copy-done, f32[3,2,64,128]{3,2,1,0:T(8,128)S(1)} %collective-permute-done.2, f32[3,2,64,128]{3,2,1,0:T(8,128)S(1)} %collective-permute-done.3, ...), kind=kLoop, calls=%fused_computation.138 | loop fusion | flops 2170880 | bytes 3702784 | tf_op jit(solution)/shard_map/reduce_sum | solution.py:89
  80.1 2.3 %add_reduce_fusion.18 = (f32[5,64,128]{2,1,0:T(8,128)}, f32[5,64,128]{2,1,0:T(8,128)}, f32[5,64,128]{2,1,0:T(8,128)}, f32[5,64,128]{2,1,0:T(8,128)}, f32[5,64,128]{2,1,0:T(8,128)S(1)}) fusion(f32[3,5,64,128]{3,2,1,0:T(8,128)S(1)} %get-tuple-element.69, f32[3,5,64,128]{3,2,1,0:T(8,128)S(1)} %get-tuple-element.68, f32[3,4,64,128]{3,2,1,0:T(8,128)S(1)} %copy-done, ...), kind=kLoop, calls=%fused_computation.134 | loop fusion | flops 2498560 | bytes 2588672 | tf_op jit(solution)/shard_map/reduce_sum | solution.py:89
  83.1 4.4 %pmax.72 = f32[]{:T(128)} all-reduce(f32[]{:T(128)} %pmax.71), channel_id=1, replica_groups=mesh['gx_0'=8,'gx_1'=4,'gy_0'=2,'gy_1'=2,'gz'=2] {'gy_0'}, use_global_device_ids=true, to_apply=%region_9.0 | all-reduce | flops 1 | bytes 8 | tf_op jit(solution)/shard_map/pmax | solution.py:21
  90.7 9.4 %pmax.73 = f32[]{:T(128)} all-reduce(f32[]{:T(128)} %pmax.72), channel_id=1, replica_groups=mesh['gx_0'=8,'gx_1'=4,'gy_0'=2,'gy_1'=2,'gz'=2] {'gy_1'}, use_global_device_ids=true, to_apply=%region_10.0 | all-reduce | flops 1 | bytes 8 | tf_op jit(solution)/shard_map/pmax | solution.py:21
  100.1 5.9 %pmax.74 = f32[]{:T(128)} all-reduce(f32[]{:T(128)} %pmax.73), channel_id=1, replica_groups=mesh['gx_0'=8,'gx_1'=4,'gy_0'=2,'gy_1'=2,'gz'=2] {'gz'}, use_global_device_ids=true, to_apply=%region_11.0 | all-reduce | flops 1 | bytes 8 | tf_op jit(solution)/shard_map/pmax | solution.py:21
  112.6 2.4 %fusion.14 = f32[6,4,64,128]{3,2,1,0:T(8,128)S(1)} fusion(f32[6,4,64,128]{3,2,1,0:T(8,128)S(1)} %bitcast_dynamic-update-slice_fusion.36, f32[6,4,64,129]{3,2,1,0:T(8,128)} %copy-done.9, f32[6,4,65,128]{3,2,1,0:T(8,128)S(1)} %bitcast_dynamic-update-slice_fusion.30, f32[6,5,64,128]{3,2,1,0:T(8,128)} %copy-done.7, f32[]{:T(128)S(6)} %div.109), kind=kLoop, calls=%fused_computation.52 | loop fusion | flops 1376256 | bytes 6291460 | tf_op jit(solution)/shard_map/sub | solution.py:149
  121.4 2.7 %collective-permute-start.17 = (f32[3,4,64,2]{3,2,1,0:T(8,128)}, f32[3,4,64,2]{3,2,1,0:T(8,128)}, u32[]{:S(2)}, u32[]{:S(2)}) collective-permute-start(f32[3,4,64,2]{3,2,1,0:T(8,128)} %get-tuple-element.93), channel_id=1, source_target_pairs={{0,2},{2,4},{4,6},{6,0},{1,3},{3,5},{5,7},{7,1},{8,10},{10,12},{12... | collective-permute-start | bytes 18440 | tf_op jit(solution)/shard_map/ppermute | solution.py:32
  125.8 12.4 %pmax.75 = f32[]{:T(128)} all-reduce(f32[]{:T(128)} %get-tuple-element.83), channel_id=1, replica_groups=mesh['gx_0'=8,'gx_1'=4,'gy_0'=2,'gy_1'=2,'gz'=2] {'gx_0'}, use_global_device_ids=true, to_apply=%region_31.32 | all-reduce | flops 1 | bytes 8 | tf_op jit(solution)/shard_map/pmax | solution.py:21
  138.9 6.8 %pmax.76 = f32[]{:T(128)} all-reduce(f32[]{:T(128)} %pmax.75), channel_id=1, replica_groups=mesh['gx_0'=8,'gx_1'=4,'gy_0'=2,'gy_1'=2,'gz'=2] {'gx_1'}, use_global_device_ids=true, to_apply=%region_32.33 | all-reduce | flops 1 | bytes 8 | tf_op jit(solution)/shard_map/pmax | solution.py:21
  146.9 4.4 %pmax.77 = f32[]{:T(128)} all-reduce(f32[]{:T(128)} %pmax.76), channel_id=1, replica_groups=mesh['gx_0'=8,'gx_1'=4,'gy_0'=2,'gy_1'=2,'gz'=2] {'gy_0'}, use_global_device_ids=true, to_apply=%region_33.34 | all-reduce | flops 1 | bytes 8 | tf_op jit(solution)/shard_map/pmax | solution.py:21
  151.3 3.5 %collective-permute-start.13 = (f32[3,2,64,128]{3,2,1,0:T(8,128)}, f32[3,2,64,128]{3,2,1,0:T(8,128)S(1)}, u32[]{:S(2)}, u32[]{:S(2)}) collective-permute-start(f32[3,2,64,128]{3,2,1,0:T(8,128)} %get-tuple-element.96), channel_id=1, source_target_pairs={{8,0},{16,8},{24,16},{32,24},{40,32},{48,40},{56,48},{64,56},{72,6... | collective-permute-start | bytes 589832 | tf_op jit(solution)/shard_map/ppermute | solution.py:33
  154.8 8.6 %pmax.78 = f32[]{:T(128)} all-reduce(f32[]{:T(128)} %pmax.77), channel_id=1, replica_groups=mesh['gx_0'=8,'gx_1'=4,'gy_0'=2,'gy_1'=2,'gz'=2] {'gy_1'}, use_global_device_ids=true, to_apply=%region_34.35 | all-reduce | flops 1 | bytes 8 | tf_op jit(solution)/shard_map/pmax | solution.py:21
  163.4 2.7 %collective-permute-start.16 = (f32[3,4,2,128]{3,2,1,0:T(2,128)}, f32[3,4,2,128]{3,2,1,0:T(2,128)}, u32[]{:S(2)}, u32[]{:S(2)}) collective-permute-start(f32[3,4,2,128]{3,2,1,0:T(2,128)} %get-tuple-element.87), channel_id=1, source_target_pairs={{0,1},{1,0},{2,3},{3,2},{4,5},{5,4},{6,7},{7,6},{8,9},{9,8},{10,11... | collective-permute-start | bytes 36872 | tf_op jit(solution)/shard_map/ppermute | solution.py:32
  167.9 5.9 %pmax.79 = f32[]{:T(128)} all-reduce(f32[]{:T(128)} %pmax.78), channel_id=1, replica_groups=mesh['gx_0'=8,'gx_1'=4,'gy_0'=2,'gy_1'=2,'gz'=2] {'gz'}, use_global_device_ids=true, to_apply=%region_35.36 | all-reduce | flops 1 | bytes 8 | tf_op jit(solution)/shard_map/pmax | solution.py:21
  179.1 4.8 %collective-permute-start.15 = (f32[3,2,64,128]{3,2,1,0:T(8,128)S(1)}, f32[3,2,64,128]{3,2,1,0:T(8,128)S(1)}, u32[]{:S(2)}, u32[]{:S(2)}) collective-permute-start(f32[3,2,64,128]{3,2,1,0:T(8,128)S(1)} %copy-done.30), channel_id=1, source_target_pairs={{8,0},{16,8},{24,16},{32,24},{40,32},{48,40},{56,48},{64,56},{72,6... | collective-permute-start | bytes 589832 | tf_op jit(solution)/shard_map/ppermute | solution.py:33
  184.8 2.8 %collective-permute-start.20 = (f32[3,4,2,128]{3,2,1,0:T(2,128)S(1)}, f32[3,4,2,128]{3,2,1,0:T(2,128)S(1)}, u32[]{:S(2)}, u32[]{:S(2)}) collective-permute-start(f32[3,4,2,128]{3,2,1,0:T(2,128)S(1)} %copy-done.33), channel_id=1, source_target_pairs={{0,1},{1,0},{2,3},{3,2},{4,5},{5,4},{6,7},{7,6},{8,9},{9,8},{10,11... | collective-permute-start | bytes 36872 | tf_op jit(solution)/shard_map/ppermute | solution.py:32
  (211 shorter events, 70.8 us)
Async XLA Ops:
  1.8 39.8 %collective-permute-start.2 = (f32[3,2,64,128]{3,2,1,0:T(8,128)S(1)}, f32[3,2,64,128]{3,2,1,0:T(8,128)S(1)}, u32[]{:S(2)}, u32[]{:S(2)}) collective-permute-start(f32[3,2,64,128]{3,2,1,0:T(8,128)S(1)} %get-tuple-element.104), channel_id=1, source_target_pairs={{0,8},{8,16},{16,24},{24,32},{32,40},{40,48},{48,56},{56,64},{64,7... | collective-permute-start | bytes 589832 | tf_op jit(solution)/shard_map/ppermute | solution.py:32
  5.0 38.0 %collective-permute-start = (f32[3,2,64,128]{3,2,1,0:T(8,128)S(1)}, f32[3,2,64,128]{3,2,1,0:T(8,128)S(1)}, u32[]{:S(2)}, u32[]{:S(2)}) collective-permute-start(f32[3,2,64,128]{3,2,1,0:T(8,128)S(1)} %get-tuple-element.110), channel_id=1, source_target_pairs={{0,8},{8,16},{16,24},{24,32},{32,40},{40,48},{48,56},{56,64},{64,7... | collective-permute-start | bytes 589832 | tf_op jit(solution)/shard_map/ppermute | solution.py:32
  6.5 10.5 %collective-permute-start.5 = (f32[3,4,64,2]{3,2,1,0:T(8,128)S(1)}, f32[3,4,64,2]{3,2,1,0:T(8,128)S(1)}, u32[]{:S(2)}, u32[]{:S(2)}) collective-permute-start(f32[3,4,64,2]{3,2,1,0:T(8,128)S(1)} %get-tuple-element.107), channel_id=1, source_target_pairs={{0,2},{2,4},{4,6},{6,0},{1,3},{3,5},{5,7},{7,1},{8,10},{10,12},{12... | collective-permute-start | bytes 18440 | tf_op jit(solution)/shard_map/ppermute | solution.py:32
  8.9 11.7 %collective-permute-start.6 = (f32[3,4,64,2]{3,2,1,0:T(8,128)S(1)}, f32[3,4,64,2]{3,2,1,0:T(8,128)S(1)}, u32[]{:S(2)}, u32[]{:S(2)}) collective-permute-start(f32[3,4,64,2]{3,2,1,0:T(8,128)S(1)} %get-tuple-element.108), channel_id=1, source_target_pairs={{2,0},{4,2},{6,4},{0,6},{3,1},{5,3},{7,5},{1,7},{10,8},{12,10},{14... | collective-permute-start | bytes 18440 | tf_op jit(solution)/shard_map/ppermute | solution.py:33
  9.1 14.0 %collective-permute-start.9 = (f32[3,4,64,2]{3,2,1,0:T(8,128)S(1)}, f32[3,4,64,2]{3,2,1,0:T(8,128)S(1)}, u32[]{:S(2)}, u32[]{:S(2)}) collective-permute-start(f32[3,4,64,2]{3,2,1,0:T(8,128)S(1)} %get-tuple-element.101), channel_id=1, source_target_pairs={{0,2},{2,4},{4,6},{6,0},{1,3},{3,5},{5,7},{7,1},{8,10},{10,12},{12... | collective-permute-start | bytes 18440 | tf_op jit(solution)/shard_map/ppermute | solution.py:32
  17.0 19.1 %collective-permute-start.4 = (f32[3,4,2,128]{3,2,1,0:T(2,128)S(1)}, f32[3,4,2,128]{3,2,1,0:T(2,128)S(1)}, u32[]{:S(2)}, u32[]{:S(2)}) collective-permute-start(f32[3,4,2,128]{3,2,1,0:T(2,128)S(1)} %get-tuple-element.99), channel_id=1, source_target_pairs={{0,1},{1,0},{2,3},{3,2},{4,5},{5,4},{6,7},{7,6},{8,9},{9,8},{10,11... | collective-permute-start | bytes 36872 | tf_op jit(solution)/shard_map/ppermute | solution.py:32
  20.6 18.0 %collective-permute-start.7 = (f32[3,4,2,128]{3,2,1,0:T(2,128)S(1)}, f32[3,4,2,128]{3,2,1,0:T(2,128)S(1)}, u32[]{:S(2)}, u32[]{:S(2)}) collective-permute-start(f32[3,4,2,128]{3,2,1,0:T(2,128)S(1)} %get-tuple-element.100), channel_id=1, source_target_pairs={{1,0},{0,1},{3,2},{2,3},{5,4},{4,5},{7,6},{6,7},{9,8},{8,9},{11,10... | collective-permute-start | bytes 36872 | tf_op jit(solution)/shard_map/ppermute | solution.py:33
  23.1 7.2 %collective-permute-start.10 = (f32[3,4,64,2]{3,2,1,0:T(8,128)S(1)}, f32[3,4,64,2]{3,2,1,0:T(8,128)S(1)}, u32[]{:S(2)}, u32[]{:S(2)}) collective-permute-start(f32[3,4,64,2]{3,2,1,0:T(8,128)S(1)} %get-tuple-element.102), channel_id=1, source_target_pairs={{2,0},{4,2},{6,4},{0,6},{3,1},{5,3},{7,5},{1,7},{10,8},{12,10},{14... | collective-permute-start | bytes 18440 | tf_op jit(solution)/shard_map/ppermute | solution.py:33
  30.3 15.2 %collective-permute-start.1 = (f32[3,2,64,128]{3,2,1,0:T(8,128)S(1)}, f32[3,2,64,128]{3,2,1,0:T(8,128)S(1)}, u32[]{:S(2)}, u32[]{:S(2)}) collective-permute-start(f32[3,2,64,128]{3,2,1,0:T(8,128)S(1)} %get-tuple-element.109), channel_id=1, source_target_pairs={{8,0},{16,8},{24,16},{32,24},{40,32},{48,40},{56,48},{64,56},{72,6... | collective-permute-start | bytes 589832 | tf_op jit(solution)/shard_map/ppermute | solution.py:33
  36.2 28.6 %collective-permute-start.3 = (f32[3,2,64,128]{3,2,1,0:T(8,128)}, f32[3,2,64,128]{3,2,1,0:T(8,128)S(1)}, u32[]{:S(2)}, u32[]{:S(2)}) collective-permute-start(f32[3,2,64,128]{3,2,1,0:T(8,128)} %get-tuple-element.103), channel_id=1, source_target_pairs={{8,0},{16,8},{24,16},{32,24},{40,32},{48,40},{56,48},{64,56},{72,6... | collective-permute-start | bytes 589832 | tf_op jit(solution)/shard_map/ppermute | solution.py:33
  38.6 48.9 %collective-permute-start.11 = (f32[3,4,2,128]{3,2,1,0:T(2,128)}, f32[3,4,2,128]{3,2,1,0:T(2,128)S(1)}, u32[]{:S(2)}, u32[]{:S(2)}) collective-permute-start(f32[3,4,2,128]{3,2,1,0:T(2,128)} %get-tuple-element.98), channel_id=1, source_target_pairs={{1,0},{0,1},{3,2},{2,3},{5,4},{4,5},{7,6},{6,7},{9,8},{8,9},{11,10... | collective-permute-start | bytes 36872 | tf_op jit(solution)/shard_map/ppermute | solution.py:33
  41.6 45.8 %collective-permute-start.8 = (f32[3,4,2,128]{3,2,1,0:T(2,128)}, f32[3,4,2,128]{3,2,1,0:T(2,128)}, u32[]{:S(2)}, u32[]{:S(2)}) collective-permute-start(f32[3,4,2,128]{3,2,1,0:T(2,128)} %get-tuple-element.97), channel_id=1, source_target_pairs={{0,1},{1,0},{2,3},{3,2},{4,5},{5,4},{6,7},{7,6},{8,9},{9,8},{10,11... | collective-permute-start | bytes 36872 | tf_op jit(solution)/shard_map/ppermute | solution.py:32
  121.4 42.1 %collective-permute-start.17 = (f32[3,4,64,2]{3,2,1,0:T(8,128)}, f32[3,4,64,2]{3,2,1,0:T(8,128)}, u32[]{:S(2)}, u32[]{:S(2)}) collective-permute-start(f32[3,4,64,2]{3,2,1,0:T(8,128)} %get-tuple-element.93), channel_id=1, source_target_pairs={{0,2},{2,4},{4,6},{6,0},{1,3},{3,5},{5,7},{7,1},{8,10},{10,12},{12... | collective-permute-start | bytes 18440 | tf_op jit(solution)/shard_map/ppermute | solution.py:32
  124.1 42.1 %collective-permute-start.18 = (f32[3,4,64,2]{3,2,1,0:T(8,128)}, f32[3,4,64,2]{3,2,1,0:T(8,128)}, u32[]{:S(2)}, u32[]{:S(2)}) collective-permute-start(f32[3,4,64,2]{3,2,1,0:T(8,128)} %get-tuple-element.94), channel_id=1, source_target_pairs={{2,0},{4,2},{6,4},{0,6},{3,1},{5,3},{7,5},{1,7},{10,8},{12,10},{14... | collective-permute-start | bytes 18440 | tf_op jit(solution)/shard_map/ppermute | solution.py:33
  124.1 42.3 %collective-permute-start.21 = (f32[3,4,64,2]{3,2,1,0:T(8,128)}, f32[3,4,64,2]{3,2,1,0:T(8,128)}, u32[]{:S(2)}, u32[]{:S(2)}) collective-permute-start(f32[3,4,64,2]{3,2,1,0:T(8,128)} %get-tuple-element.89), channel_id=1, source_target_pairs={{0,2},{2,4},{4,6},{6,0},{1,3},{3,5},{5,7},{7,1},{8,10},{10,12},{12... | collective-permute-start | bytes 18440 | tf_op jit(solution)/shard_map/ppermute | solution.py:32
  145.6 42.8 %collective-permute-start.12 = (f32[3,2,64,128]{3,2,1,0:T(8,128)}, f32[3,2,64,128]{3,2,1,0:T(8,128)S(1)}, u32[]{:S(2)}, u32[]{:S(2)}) collective-permute-start(f32[3,2,64,128]{3,2,1,0:T(8,128)} %get-tuple-element.95), channel_id=1, source_target_pairs={{0,8},{8,16},{16,24},{24,32},{32,40},{40,48},{48,56},{56,64},{64,7... | collective-permute-start | bytes 589832 | tf_op jit(solution)/shard_map/ppermute | solution.py:32
  151.3 37.7 %collective-permute-start.13 = (f32[3,2,64,128]{3,2,1,0:T(8,128)}, f32[3,2,64,128]{3,2,1,0:T(8,128)S(1)}, u32[]{:S(2)}, u32[]{:S(2)}) collective-permute-start(f32[3,2,64,128]{3,2,1,0:T(8,128)} %get-tuple-element.96), channel_id=1, source_target_pairs={{8,0},{16,8},{24,16},{32,24},{40,32},{48,40},{56,48},{64,56},{72,6... | collective-permute-start | bytes 589832 | tf_op jit(solution)/shard_map/ppermute | solution.py:33
  163.4 15.7 %collective-permute-start.16 = (f32[3,4,2,128]{3,2,1,0:T(2,128)}, f32[3,4,2,128]{3,2,1,0:T(2,128)}, u32[]{:S(2)}, u32[]{:S(2)}) collective-permute-start(f32[3,4,2,128]{3,2,1,0:T(2,128)} %get-tuple-element.87), channel_id=1, source_target_pairs={{0,1},{1,0},{2,3},{3,2},{4,5},{5,4},{6,7},{7,6},{8,9},{9,8},{10,11... | collective-permute-start | bytes 36872 | tf_op jit(solution)/shard_map/ppermute | solution.py:32
  166.2 18.6 %collective-permute-start.19 = (f32[3,4,2,128]{3,2,1,0:T(2,128)S(1)}, f32[3,4,2,128]{3,2,1,0:T(2,128)}, u32[]{:S(2)}, u32[]{:S(2)}) collective-permute-start(f32[3,4,2,128]{3,2,1,0:T(2,128)S(1)} %get-tuple-element.88), channel_id=1, source_target_pairs={{1,0},{0,1},{3,2},{2,3},{5,4},{4,5},{7,6},{6,7},{9,8},{8,9},{11,10... | collective-permute-start | bytes 36872 | tf_op jit(solution)/shard_map/ppermute | solution.py:33
  166.4 11.5 %collective-permute-start.22 = (f32[3,4,64,2]{3,2,1,0:T(8,128)S(1)}, f32[3,4,64,2]{3,2,1,0:T(8,128)}, u32[]{:S(2)}, u32[]{:S(2)}) collective-permute-start(f32[3,4,64,2]{3,2,1,0:T(8,128)S(1)} %get-tuple-element.90), channel_id=1, source_target_pairs={{2,0},{4,2},{6,4},{0,6},{3,1},{5,3},{7,5},{1,7},{10,8},{12,10},{14... | collective-permute-start | bytes 18440 | tf_op jit(solution)/shard_map/ppermute | solution.py:33
  177.9 12.8 %collective-permute-start.14 = (f32[3,2,64,128]{3,2,1,0:T(8,128)S(1)}, f32[3,2,64,128]{3,2,1,0:T(8,128)S(1)}, u32[]{:S(2)}, u32[]{:S(2)}) collective-permute-start(f32[3,2,64,128]{3,2,1,0:T(8,128)S(1)} %copy-done.31), channel_id=1, source_target_pairs={{0,8},{8,16},{16,24},{24,32},{32,40},{40,48},{48,56},{56,64},{64,7... | collective-permute-start | bytes 589832 | tf_op jit(solution)/shard_map/ppermute | solution.py:32
  179.1 11.6 %collective-permute-start.15 = (f32[3,2,64,128]{3,2,1,0:T(8,128)S(1)}, f32[3,2,64,128]{3,2,1,0:T(8,128)S(1)}, u32[]{:S(2)}, u32[]{:S(2)}) collective-permute-start(f32[3,2,64,128]{3,2,1,0:T(8,128)S(1)} %copy-done.30), channel_id=1, source_target_pairs={{8,0},{16,8},{24,16},{32,24},{40,32},{48,40},{56,48},{64,56},{72,6... | collective-permute-start | bytes 589832 | tf_op jit(solution)/shard_map/ppermute | solution.py:33
  184.8 6.6 %collective-permute-start.20 = (f32[3,4,2,128]{3,2,1,0:T(2,128)S(1)}, f32[3,4,2,128]{3,2,1,0:T(2,128)S(1)}, u32[]{:S(2)}, u32[]{:S(2)}) collective-permute-start(f32[3,4,2,128]{3,2,1,0:T(2,128)S(1)} %copy-done.33), channel_id=1, source_target_pairs={{0,1},{1,0},{2,3},{3,2},{4,5},{5,4},{6,7},{7,6},{8,9},{9,8},{10,11... | collective-permute-start | bytes 36872 | tf_op jit(solution)/shard_map/ppermute | solution.py:32
  188.4 4.4 %collective-permute-start.23 = (f32[3,4,2,128]{3,2,1,0:T(2,128)S(1)}, f32[3,4,2,128]{3,2,1,0:T(2,128)S(1)}, u32[]{:S(2)}, u32[]{:S(2)}) collective-permute-start(f32[3,4,2,128]{3,2,1,0:T(2,128)S(1)} %copy-done.32), channel_id=1, source_target_pairs={{1,0},{0,1},{3,2},{2,3},{5,4},{4,5},{7,6},{6,7},{9,8},{8,9},{11,10... | collective-permute-start | bytes 36872 | tf_op jit(solution)/shard_map/ppermute | solution.py:33
  (34 other events, 230.6 us)
where the time goes:
time: 200 us; the launch traced here: 198 us
  blocking collectives  78.6 us (39%)
  starting transfers between devices  43.9 us (22%)
  other arithmetic  32.6 us (16%)
  local copies, waits for them, and re-layouts  27.4 us (14%)
  waiting for transfers between devices  13.5 us (7%)
  between operations  2.27 us (1%)
    pmax x10, blocking collectives, by_axis(): return functools.reduce(lax.pmax, axes, value)  78.6 us
    ppermute x12, starting transfers between devices, extended(): lax.ppermute(last, axis, up)  22 us
    ppermute x12, starting transfers between devices, extended(): lax.ppermute(initial, axis, [(b, a) for a, b in up])  21.9 us
    unnamed x105, local copies, waits for them, and re-layouts  9.23 us
    reduce_sum x8, other arithmetic, face_divergence(): fluxes.append(jnp.sum(left_term + right_term, axis=0))  9.13 us
    ppermute x12, waiting for transfers between devices, extended(): lax.ppermute(initial, axis, [(b, a) for a, b in up])  7.36 us
    ppermute x12, waiting for transfers between devices, extended(): lax.ppermute(last, axis, up)  6.11 us
    mul x4, other arithmetic, face_divergence(): left_term = component * left_w * jnp.maximum(left_u, 0.0)  5.08 us
  transfers between devices with their start and end apart: 24, of which 4 were waited for; matrix products, arithmetic and copies ran while one was open for 17% of the time, Pallas kernels for 0%

commit v1 on v0

v1 whole, which is shorter than its diff:
```python
import math

import numpy as np
import jax
import jax.numpy as jnp
from jax import lax
from jax.experimental import pallas as pl
from jax.experimental.pallas import tpu as pltpu
from jax.sharding import PartitionSpec as P

AXES = ("gx", "gy", "gz")
COURANT = 0.4
SPEED_TOTAL = 1.72
SPEED_X, SPEED_Z, SPEED_Y = 0.6, 0.64, 0.48
ROWS = 8


def root_table(degree):
    points = np.cos((np.arange(400) + 0.5) * np.pi / 400)
    values = np.cos(2.0 / 3.0 * np.arccos(0.5 * (points + 1.0)))
    fit = np.polynomial.chebyshev.Chebyshev.fit(points, values, degree, domain=[-1, 1])
    return [float(c) for c in fit.convert(kind=np.polynomial.Polynomial).coef]


ROOT = root_table(11)


def cos_third(ratio):
    half = jnp.sqrt(jnp.maximum(0.5 + 0.5 * ratio, 0.0))
    t = 2.0 * half - 1.0
    total = jnp.full_like(t, ROOT[-1])
    for c in ROOT[-2::-1]:
        total = total * t + c
    return total


def limited(a, b):
    return jnp.maximum(jnp.minimum(a, b), 0.0) + jnp.minimum(jnp.maximum(a, b), 0.0)


def side_terms(c, wm2, wm1, w, wp1, wp2, um1, u, up1):
    d0, d1, d2, d3 = wm1 - wm2, w - wm1, wp1 - w, wp2 - wp1
    below = limited(d0, d1)
    here = (0.5 * c) * limited(d1, d2)
    above = limited(d2, d3)
    base = c * w
    own = (base + here) * jnp.maximum(u, 0.0) - (base - here) * jnp.minimum(u, 0.0)
    low = (wm1 + 0.5 * below) * (c * jnp.minimum(-um1, 0.0))
    high = (wp1 - 0.5 * above) * (c * jnp.minimum(up1, 0.0))
    return own, low, high


class Fields:
    def __init__(self, w, u, pw, pu, xlo, xhi, ylo, yhi):
        self.w, self.u, self.pw, self.pu = w, u, pw, pu
        self.xlo, self.xhi, self.ylo, self.yhi = xlo, xhi, ylo, yhi

    def plane_w(self, n, x, z):
        if x == -1:
            return self.xlo[n, z, :]
        if x == -2:
            return self.xlo[6 + n, z, :]
        if x == 4:
            return self.xhi[n, z, :]
        if x == 5:
            return self.xhi[6 + n, z, :]
        return self.w[n, x, z, :]

    def plane_u(self, n, x, z):
        if x == -1:
            return self.xlo[3 + n, z, :]
        if x == 4:
            return self.xhi[3 + n, z, :]
        return self.u[n, x, z, :]


def pad_rows(f, zr):
    def copy(i, carry):
        z = pl.ds(pl.multiple_of(i * ROWS, ROWS), ROWS)
        zp = pl.ds(pl.multiple_of(i * ROWS + 8, ROWS), ROWS)
        f.pw[:, :, zp, :] = f.w[:, :, z, :]
        f.pu[:, :, zp, :] = f.u[:, :, z, :]
        return carry

    lax.fori_loop(0, 64 // ROWS, copy, 0)
    f.pw[:, :, 7, :] = zr[0, 0:3]
    f.pu[:, :, 7, :] = zr[0, 3:6]
    f.pw[:, :, 6, :] = zr[0, 6:9]
    f.pw[:, :, 72, :] = zr[1, 0:3]
    f.pu[:, :, 72, :] = zr[1, 3:6]
    f.pw[:, :, 73, :] = zr[1, 6:9]


def divergence(f, i, x, lane):
    z0 = i * ROWS
    z = pl.ds(pl.multiple_of(z0, ROWS), ROWS)
    first, final = lane == 0, lane == 127
    hlo, hhi = f.ylo[z, :], f.yhi[z, :]

    def halo_lo(k):
        return pltpu.roll(hlo, (128 - (4 * k + x)) % 128, 1)

    def halo_hi(k):
        return pltpu.roll(hhi, 127 - (4 * k + x), 1)

    total = [None] * 6
    nodes = []
    for n in range(3):
        w, u = f.w[n, x, z, :], f.u[n, x, z, :]
        nodes.append((w, u))
        parts = []
        um1, up1 = f.plane_u(n, x - 1, z), f.plane_u(n, x + 1, z)
        own, low, high = side_terms(
            SPEED_X, *[f.plane_w(n, x + s, z) for s in (-2, -1)], w,
            *[f.plane_w(n, x + s, z) for s in (1, 2)], um1, u, up1)
        parts += [(low, um1), (high, up1)]

        def row_w(s):
            return f.pw[n, x, pl.ds(z0 + 8 + s, ROWS), :]

        um1, up1 = f.pu[n, x, pl.ds(z0 + 7, ROWS), :], f.pu[n, x, pl.ds(z0 + 9, ROWS), :]
        own_z, low, high = side_terms(
            SPEED_Z, row_w(-2), row_w(-1), w, row_w(1), row_w(2), um1, u, up1)
        parts += [(low, um1), (high, up1)]
        own = own + own_z
        um1 = jnp.where(first, halo_lo(3 + n), pltpu.roll(u, 1, 1))
        up1 = jnp.where(final, halo_hi(3 + n), pltpu.roll(u, 127, 1))
        wm1 = jnp.where(first, halo_lo(n), pltpu.roll(w, 1, 1))
        wp1 = jnp.where(final, halo_hi(n), pltpu.roll(w, 127, 1))
        wm2 = jnp.where(first, halo_lo(6 + n), pltpu.roll(wm1, 1, 1))
        wp2 = jnp.where(final, halo_hi(6 + n), pltpu.roll(wp1, 127, 1))
        own_y, low, high = side_terms(SPEED_Y, wm2, wm1, w, wp1, wp2, um1, u, up1)
        parts += [(low, um1), (high, up1)]
        own = own + own_y
        parts.append((own, u))
        for order in range(6):
            term = parts[0][0]
            for value, _ in parts[1:]:
                term = term + value
            total[order] = term if total[order] is None else total[order] + term
            if order < 5:
                parts = [(value * speed, speed) for value, speed in parts]
    return total, nodes


def moments_of(nodes):
    total = [None] * 6
    for w, u in nodes:
        power = w
        for order in range(6):
            total[order] = power if total[order] is None else total[order] + power
            if order < 5:
                power = power * u
    return total


def invert(mom):
    inv0 = 1.0 / mom[0]
    a0 = mom[1] * inv0
    s1 = [None] + [mom[l + 1] - a0 * mom[l] for l in range(1, 5)]
    inv1 = 1.0 / s1[1]
    quot = s1[2] * inv1
    a1 = quot - a0
    b1 = s1[1] * inv0
    s2_two = s1[3] - a1 * s1[2] - b1 * mom[2]
    s2_three = s1[4] - a1 * s1[3] - b1 * mom[3]
    a2 = s2_three / s2_two - quot
    b2 = s2_two * inv1
    q = (a0 + a1 + a2) * (1.0 / 3.0)
    d0, d1, d2 = a0 - q, a1 - q, a2 - q
    square = (d0 * d0 + d1 * d1 + d2 * d2 + 2.0 * b1 + 2.0 * b2) * (1.0 / 6.0)
    p = jnp.sqrt(square)
    det = d0 * d1 * d2 - d0 * b2 - d2 * b1
    ratio = det / (2.0 * square * p)
    high = q + 2.0 * p * cos_third(ratio)
    low = q - 2.0 * p * cos_third(-ratio)
    middle = 3.0 * q - high - low
    both = b1 * b2
    scale = mom[0] * both
    nodes = []
    for value in (low, middle, high):
        e0 = value - a0
        e1 = (value - a1) * e0 - b1
        nodes.append((scale / (both + b2 * (e0 * e0) + e1 * e1), value))
    return nodes


def write_sides(w, u, xup, xdn, yup, ydn, zs, lane):
    zs[0, 0:3] = w[:, :, 63, :]
    zs[0, 3:6] = u[:, :, 63, :]
    zs[0, 6:9] = w[:, :, 62, :]
    zs[1, 0:3] = w[:, :, 0, :]
    zs[1, 3:6] = u[:, :, 0, :]
    zs[1, 6:9] = w[:, :, 1, :]

    def rows(i, carry):
        z = pl.ds(pl.multiple_of(i * ROWS, ROWS), ROWS)
        xup[0:3, z, :] = w[:, 3, z, :]
        xup[3:6, z, :] = u[:, 3, z, :]
        xup[6:9, z, :] = w[:, 2, z, :]
        xdn[0:3, z, :] = w[:, 0, z, :]
        xdn[3:6, z, :] = u[:, 0, z, :]
        xdn[6:9, z, :] = w[:, 1, z, :]
        up = jnp.zeros((ROWS, 128), jnp.float32)
        dn = up
        for n in range(3):
            for x in range(4):
                vw, vu = w[n, x, z, :], u[n, x, z, :]
                for k, value, ahead, back in ((n, vw, 127, 0), (3 + n, vu, 127, 0), (6 + n, vw, 126, 1)):
                    at = 4 * k + x
                    up = jnp.where(lane == at, pltpu.roll(value, (at - ahead) % 128, 1), up)
                    dn = jnp.where(lane == at, pltpu.roll(value, (at - back) % 128, 1), dn)
        yup[z, :] = up
        ydn[z, :] = dn
        return carry

    lax.fori_loop(0, 64 // ROWS, rows, 0)


def lanes():
    return lax.broadcasted_iota(jnp.int32, (ROWS, 128), 1)


def write_top(top, mx):
    mx[...] = jnp.full(mx.shape, jnp.max(top), jnp.float32)


def step_of(received):
    top = jnp.max(received[...], axis=0, keepdims=True)
    return COURANT / (SPEED_TOTAL * top)


def entry_kernel(w, u, xup, xdn, yup, ydn, zs, mx):
    top = jnp.zeros((ROWS, 128), jnp.float32)
    for x in range(4):
        for i in range(64 // ROWS):
            z = slice(i * ROWS, (i + 1) * ROWS)
            top = jnp.maximum(top, jnp.maximum(jnp.abs(u[0, x, z, :]), jnp.maximum(jnp.abs(u[1, x, z, :]), jnp.abs(u[2, x, z, :]))))
    write_top(top, mx)
    write_sides(w, u, xup, xdn, yup, ydn, zs, lanes())


def middle_kernel(w, u, xlo, xhi, ylo, yhi, zr, got, base, mw, mu, xup, xdn, yup, ydn, zs, mx, pw, pu):
    f = Fields(w, u, pw, pu, xlo, xhi, ylo, yhi)
    pad_rows(f, zr)
    step = step_of(got)
    lane = lanes()

    def rows(i, top):
        z = pl.ds(pl.multiple_of(i * ROWS, ROWS), ROWS)
        for x in range(4):
            change, nodes = divergence(f, i, x, lane)
            start = moments_of(nodes)
            mid = [s - step * d for s, d in zip(start, change)]
            for k in range(6):
                base[k, x, z, :] = 0.5 * (start[k] + mid[k])
            for n, (weight, speed) in enumerate(invert(mid)):
                mw[n, x, z, :] = weight
                mu[n, x, z, :] = speed
                top = jnp.maximum(top, jnp.abs(speed))
        return top

    top = lax.fori_loop(0, 64 // ROWS, rows, jnp.zeros((ROWS, 128), jnp.float32))
    write_top(top, mx)
    write_sides(mw, mu, xup, xdn, yup, ydn, zs, lane)


def exit_kernel(w, u, xlo, xhi, ylo, yhi, zr, got, base, out, pw, pu):
    f = Fields(w, u, pw, pu, xlo, xhi, ylo, yhi)
    pad_rows(f, zr)
    half = 0.5 * step_of(got)
    lane = lanes()

    def rows(i, carry):
        z = pl.ds(pl.multiple_of(i * ROWS, ROWS), ROWS)
        for x in range(4):
            change, _ = divergence(f, i, x, lane)
            for k in range(6):
                out[k, x, z, :] = base[k, x, z, :] - half * change[k]
        return carry

    lax.fori_loop(0, 64 // ROWS, rows, 0)


def f32(*shape):
    return jax.ShapeDtypeStruct(shape, jnp.float32)


SIDES = (f32(9, 64, 128), f32(9, 64, 128), f32(64, 128), f32(64, 128), f32(2, 9, 4, 128))
NODES = (f32(3, 4, 64, 128), f32(3, 4, 64, 128))
PADDED = [pltpu.VMEM((3, 4, 80, 128), jnp.float32)] * 2


def call(kernel, outs, args, scratch=()):
    spec = pl.BlockSpec(memory_space=pltpu.VMEM)
    return pl.pallas_call(
        kernel,
        out_shape=outs,
        in_specs=[spec] * len(args),
        out_specs=jax.tree.map(lambda _: spec, outs),
        scratch_shapes=list(scratch),
        compiler_params=pltpu.CompilerParams(vmem_limit_bytes=24 * 1024 * 1024),
    )(*args)


def local(weights, abscissas):
    nx, ny, nz = (lax.axis_size(a) for a in AXES)
    everyone = nx * ny * nz

    def ring(n, s):
        return [(i, (i + s) % n) for i in range(n)]

    def exchange(xup, xdn, yup, ydn, zs):
        return (
            lax.ppermute(xup, "gx", ring(nx, 1)),
            lax.ppermute(xdn, "gx", ring(nx, -1)),
            lax.ppermute(yup, "gy", ring(ny, 1)),
            lax.ppermute(ydn, "gy", ring(ny, -1)),
            lax.ppermute(zs, "gz", ring(nz, 1)),
        )

    def spread(top):
        return lax.all_to_all(top.reshape(everyone, 1, 128), AXES, 0, 0).reshape(everyone, 128)

    tops = f32(everyone, 128)
    *sides, top = call(entry_kernel, SIDES + (tops,), (weights, abscissas))
    halo = exchange(*sides)
    got = spread(top)
    base, mw, mu, *sides, top = call(
        middle_kernel, (f32(6, 4, 64, 128),) + NODES + SIDES + (tops,),
        (weights, abscissas, *halo, got), PADDED)
    halo = exchange(*sides)
    got = spread(top)
    return call(exit_kernel, f32(6, 4, 64, 128), (mw, mu, *halo, got, base), PADDED)


def solution(mesh):
    spec = P(None, "gx", "gz", "gy")
    return jax.shard_map(local, mesh=mesh, in_specs=(spec, spec), out_specs=spec, check_vma=False)
```

time: 200 us -> 71.2 us (0.36)
  blocking collectives: 78.6 us -> 0 us
  other arithmetic: 32.6 us -> 0 us
  local copies, waits for them, and re-layouts: 27.4 us -> 2.6 us
  Pallas kernels: 0 us -> 13.2 us
  starting transfers between devices: 43.9 us -> 37.2 us
  waiting for transfers between devices: 13.5 us -> 17.9 us
  between operations: 2.27 us -> 0.05 us
    pmax x10 -> x0, blocking collectives: 78.6 us -> none  [by_axis(): return functools.reduce(lax.pmax, axes, value)]
    ppermute x24 -> x10, starting transfers between devices: 43.9 us -> 21.3 us  [the longest x2 11.2 us: exchange(): lax.ppermute(xdn, 'gx', ring(nx, -1))]
    all_to_all x0 -> x2, starting transfers between devices: none -> 15.9 us  [spread(): lax.all_to_all(top.reshape(everyone, 1, 128), AXES, 0, 0)]
    pallas_call x0 -> x3, Pallas kernels: none -> 13.2 us  [call(): pl.pallas_call(kernel, out_shape=outs, in_specs=[spec] * len(args), out_s...]
    reduce_sum x9 -> x0, other arithmetic: 11 us -> none  [the longest x8 9.13 us: face_divergence(): fluxes.append(jnp.sum(left_term + right_term, axis=0))]
    all_to_all x0 -> x2, waiting for transfers between devices: none -> 10.3 us  [spread(): lax.all_to_all(top.reshape(everyone, 1, 128), AXES, 0, 0)]
    pad x12 -> x0, local copies, waits for them, and re-layouts: 9.46 us -> none  [the longest x6 4.74 us: extended(): jnp.pad(low, around)]
    slice x11 -> x0, local copies, waits for them, and re-layouts: 7.88 us -> none  [the longest x9 5.04 us: extended(): last = lax.slice_in_dim(value, length - width, length, axis=dim)]
  transfers between devices with their start and end apart: 24 -> 12, of which waited for: 4 -> 6; matrix products, arithmetic and copies ran while one was open for 17% -> 0% of each run, Pallas kernels for 0% -> 0%
where the time goes in v1:
time: 71.2 us; the launch traced here: 70.9 us
  starting transfers between devices  37.2 us (52%)
  waiting for transfers between devices  17.9 us (25%)
  Pallas kernels  13.2 us (19%)
  local copies, waits for them, and re-layouts  2.6 us (4%)
    all_to_all x2, starting transfers between devices, spread(): lax.all_to_all(top.reshape(everyone, 1, 128), AXES, 0, 0)  15.9 us
    pallas_call x3, Pallas kernels, call(): pl.pallas_call(kernel, out_shape=outs, in_specs=[spec] * len(args), out_s...  13.2 us
    ppermute x2, starting transfers between devices, exchange(): lax.ppermute(xdn, 'gx', ring(nx, -1))  11.2 us
    all_to_all x2, waiting for transfers between devices, spread(): lax.all_to_all(top.reshape(everyone, 1, 128), AXES, 0, 0)  10.3 us
    ppermute x2, starting transfers between devices, exchange(): lax.ppermute(zs, 'gz', ring(nz, 1))  5.92 us
    ppermute x2, waiting for transfers between devices, exchange(): lax.ppermute(ydn, 'gy', ring(ny, -1))  5.11 us
    unnamed x12, local copies, waits for them, and re-layouts  2.6 us
    ppermute x2, starting transfers between devices, exchange(): lax.ppermute(xup, 'gx', ring(nx, 1))  2.47 us
  transfers between devices with their start and end apart: 12, of which 6 were waited for; matrix products, arithmetic and copies ran while one was open for 0% of the time, Pallas kernels for 0%

profile of v1, /device:TPU:1, one launch (start us, length us, event | category | flops | bytes accessed | tf_op | source)
XLA Modules:
  0.0 70.9 jit_solution(6675353406225478062)
XLA Ops:
  0.0 1.0 %copy-done = f32[3,4,64,128]{3,2,1,0:T(8,128)S(1)} copy-done((f32[3,4,64,128]{3,2,1,0:T(8,128)S(1)}, f32[3,4,64,128]{3,2,1,0:T(8,128)}, u32[]{:S(2)}) %copy-start) | copy-done | bytes 393240
  1.0 1.0 %copy-done.2 = f32[3,4,64,128]{3,2,1,0:T(8,128)S(1)} copy-done((f32[3,4,64,128]{3,2,1,0:T(8,128)S(1)}, f32[3,4,64,128]{3,2,1,0:T(8,128)}, u32[]{:S(2)}) %copy-start.2) | copy-done | bytes 393240
  2.0 1.9 %shard_map.28 = (f32[9,64,128]{2,1,0:T(8,128)S(1)}, f32[9,64,128]{2,1,0:T(8,128)S(1)}, f32[64,128]{1,0:T(8,128)S(1)}, f32[64,128]{1,0:T(8,128)S(1)}, f32[2,9,4,128]{3,2,1,0:T(4,128)S(1)}, /*index=5*/f32[256,128]{1,0:T(8,128)}) custom-call(f32[3,4,64,128]{3,2,1,0:T(8,128)S(1)} %copy-done, f32[3,4,64,128]{3,2,1,0:T(8,128)S(1)} %copy-done.2), custom_call_target="tpu_custom_call" | custom-call | tf_op jit(solution)/shard_map/pallas_call | solution.py:296
  3.9 2.1 %collective-permute-start = (f32[9,64,128]{2,1,0:T(8,128)S(1)}, f32[9,64,128]{2,1,0:T(8,128)S(1)}, u32[]{:S(2)}, u32[]{:S(2)}) collective-permute-start(f32[9,64,128]{2,1,0:T(8,128)S(1)} %get-tuple-element.20), channel_id=1, source_target_pairs={{0,8},{8,16},{16,24},{24,32},{32,40},{40,48},{48,56},{56,64},{64,7... | collective-permute-start | bytes 884744 | tf_op jit(solution)/shard_map/ppermute | solution.py:315
  6.0 6.7 %collective-permute-start.1 = (f32[9,64,128]{2,1,0:T(8,128)S(1)}, f32[9,64,128]{2,1,0:T(8,128)S(1)}, u32[]{:S(2)}, u32[]{:S(2)}) collective-permute-start(f32[9,64,128]{2,1,0:T(8,128)S(1)} %get-tuple-element.21), channel_id=1, source_target_pairs={{0,248},{8,0},{16,8},{24,16},{32,24},{40,32},{48,40},{56,48},{64,5... | collective-permute-start | bytes 884744 | tf_op jit(solution)/shard_map/ppermute | solution.py:316
  12.8 9.5 %all-to-all-start = ((f32[256,1,128]{2,1,0:T(1,128)}), f32[256,1,128]{2,1,0:T(1,128)S(1)}, u32[]{:S(2)}, u32[]{:S(2)}) async-start(f32[256,1,128]{2,1,0:T(1,128)} %bitcast.1), calls=%async_computation | async-start | bytes 262144 | tf_op jit(solution)/shard_map/all_to_all | solution.py:323
  22.3 2.9 %collective-permute-start.4 = (f32[2,9,4,128]{3,2,1,0:T(4,128)S(1)}, f32[2,9,4,128]{3,2,1,0:T(4,128)S(1)}, u32[]{:S(2)}, u32[]{:S(2)}) collective-permute-start(f32[2,9,4,128]{3,2,1,0:T(4,128)S(1)} %get-tuple-element.24), channel_id=1, source_target_pairs={{0,1},{1,0},{2,3},{3,2},{4,5},{5,4},{6,7},{7,6},{8,9},{9,8},{10,11... | collective-permute-start | bytes 110600 | tf_op jit(solution)/shard_map/ppermute | solution.py:319
  25.2 0.8 %collective-permute-start.2 = (f32[64,128]{1,0:T(8,128)S(1)}, f32[64,128]{1,0:T(8,128)S(1)}, u32[]{:S(2)}, u32[]{:S(2)}) collective-permute-start(f32[64,128]{1,0:T(8,128)S(1)} %get-tuple-element.22), channel_id=1, source_target_pairs={{0,2},{2,4},{4,6},{6,0},{1,3},{3,5},{5,7},{7,1},{8,10},{10,12},{12... | collective-permute-start | bytes 98312 | tf_op jit(solution)/shard_map/ppermute | solution.py:317
  26.1 0.0 collective-permute-start.3
  26.1 1.2 %collective-permute-done.2.ylo = f32[64,128]{1,0:T(8,128)S(1)} collective-permute-done((f32[64,128]{1,0:T(8,128)S(1)}, f32[64,128]{1,0:T(8,128)S(1)}, u32[]{:S(2)}, u32[]{:S(2)}) %collective-permute-start.2) | collective-permute-done | bytes 32800 | tf_op jit(solution)/shard_map/ppermute | solution.py:317
  27.3 2.5 %collective-permute-done.3.yhi = f32[64,128]{1,0:T(8,128)S(1)} collective-permute-done((f32[64,128]{1,0:T(8,128)S(1)}, f32[64,128]{1,0:T(8,128)S(1)}, u32[]{:S(2)}, u32[]{:S(2)}) %collective-permute-start.3) | collective-permute-done | bytes 32800 | tf_op jit(solution)/shard_map/ppermute | solution.py:318
  29.8 5.1 %all-to-all-done = f32[256,1,128]{2,1,0:T(1,128)S(1)} async-done(((f32[256,1,128]{2,1,0:T(1,128)}), f32[256,1,128]{2,1,0:T(1,128)S(1)}, u32[]{:S(2)}, u32[]{:S(2)}) %all-to-all-start) | async-done | bytes 131104 | tf_op jit(solution)/shard_map/all_to_all | solution.py:323
  34.9 0.0 collective-permute-done.1.xhi
  35.0 7.1 %shard_map.29 = (f32[6,4,64,128]{3,2,1,0:T(8,128)S(1)}, f32[3,4,64,128]{3,2,1,0:T(8,128)S(1)}, f32[3,4,64,128]{3,2,1,0:T(8,128)S(1)}, f32[9,64,128]{2,1,0:T(8,12...) custom-call(f32[3,4,64,128]{3,2,1,0:T(8,128)S(1)} %copy-done.1, ...), custom_call_target="tpu_custom_call" | custom-call | tf_op jit(solution)/shard_map/pallas_call | solution.py:296
  42.1 0.6 copy-done.4
  42.7 0.4 collective-permute-start.5
  43.0 4.4 %collective-permute-start.6 = (f32[9,64,128]{2,1,0:T(8,128)S(1)}, f32[9,64,128]{2,1,0:T(8,128)S(1)}, u32[]{:S(2)}, u32[]{:S(2)}) collective-permute-start(f32[9,64,128]{2,1,0:T(8,128)S(1)} %get-tuple-element.29), channel_id=1, source_target_pairs={{0,248},{8,0},{16,8},{24,16},{32,24},{40,32},{48,40},{56,48},{64,5... | collective-permute-start | bytes 884744 | tf_op jit(solution)/shard_map/ppermute | solution.py:316
  47.4 6.4 %all-to-all-start.1 = ((f32[256,1,128]{2,1,0:T(1,128)}), f32[256,1,128]{2,1,0:T(1,128)S(1)}, u32[]{:S(2)}, u32[]{:S(2)}) async-start(f32[256,1,128]{2,1,0:T(1,128)} %bitcast.4), calls=%async_computation.1 | async-start | bytes 262144 | tf_op jit(solution)/shard_map/all_to_all | solution.py:323
  53.9 3.0 %collective-permute-start.9 = (f32[2,9,4,128]{3,2,1,0:T(4,128)S(1)}, f32[2,9,4,128]{3,2,1,0:T(4,128)S(1)}, u32[]{:S(2)}, u32[]{:S(2)}) collective-permute-start(f32[2,9,4,128]{3,2,1,0:T(4,128)S(1)} %get-tuple-element.32), channel_id=1, source_target_pairs={{0,1},{1,0},{2,3},{3,2},{4,5},{5,4},{6,7},{7,6},{8,9},{9,8},{10,11... | collective-permute-start | bytes 110600 | tf_op jit(solution)/shard_map/ppermute | solution.py:319
  56.9 0.9 %collective-permute-start.7 = (f32[64,128]{1,0:T(8,128)S(1)}, f32[64,128]{1,0:T(8,128)S(1)}, u32[]{:S(2)}, u32[]{:S(2)}) collective-permute-start(f32[64,128]{1,0:T(8,128)S(1)} %copy-done.5), channel_id=1, source_target_pairs={{0,2},{2,4},{4,6},{6,0},{1,3},{3,5},{5,7},{7,1},{8,10},{10,12},{12... | collective-permute-start | bytes 98312 | tf_op jit(solution)/shard_map/ppermute | solution.py:317
  57.7 1.2 %collective-permute-done.7.ylo = f32[64,128]{1,0:T(8,128)S(1)} collective-permute-done((f32[64,128]{1,0:T(8,128)S(1)}, f32[64,128]{1,0:T(8,128)S(1)}, u32[]{:S(2)}, u32[]{:S(2)}) %collective-permute-start.7) | collective-permute-done | bytes 32800 | tf_op jit(solution)/shard_map/ppermute | solution.py:317
  58.9 2.6 %collective-permute-done.8.yhi = f32[64,128]{1,0:T(8,128)S(1)} collective-permute-done((f32[64,128]{1,0:T(8,128)S(1)}, f32[64,128]{1,0:T(8,128)S(1)}, u32[]{:S(2)}, u32[]{:S(2)}) %collective-permute-start.8) | collective-permute-done | bytes 32800 | tf_op jit(solution)/shard_map/ppermute | solution.py:318
  61.5 5.2 %all-to-all-done.1 = f32[256,1,128]{2,1,0:T(1,128)S(1)} async-done(((f32[256,1,128]{2,1,0:T(1,128)}), f32[256,1,128]{2,1,0:T(1,128)S(1)}, u32[]{:S(2)}, u32[]{:S(2)}) %all-to-all-start.1) | async-done | bytes 131104 | tf_op jit(solution)/shard_map/all_to_all | solution.py:323
  66.7 4.2 %shard_map.30 = f32[6,4,64,128]{3,2,1,0:T(8,128)} custom-call(f32[3,4,64,128]{3,2,1,0:T(8,128)S(1)} %get-tuple-element.26.w, f32[3,4,64,128]{3,2,1,0:T(8,128)S(1)} %get-tuple-element.27.u, f32[9,64,128]{2,1,0:T(8,128)S(1)} %collective-permute-done.5.xlo, f32[9,64,128]{2,1,0:T(8,128)S(1)} %collective-permute-done.6.xhi, ...), custom_call_target="tpu_custom_call" | custom-call | tf_op jit(solution)/shard_map/pallas_call | solution.py:296
  (15 shorter events, 0.0 us)
Async XLA Ops:
  0.0 1.0 %copy-start = (f32[3,4,64,128]{3,2,1,0:T(8,128)S(1)}, f32[3,4,64,128]{3,2,1,0:T(8,128)}, u32[]{:S(2)}) copy-start(f32[3,4,64,128]{3,2,1,0:T(8,128)} %w.3) | copy-start | bytes 1179652
  1.0 1.0 %copy-start.2 = (f32[3,4,64,128]{3,2,1,0:T(8,128)S(1)}, f32[3,4,64,128]{3,2,1,0:T(8,128)}, u32[]{:S(2)}) copy-start(f32[3,4,64,128]{3,2,1,0:T(8,128)} %u.3) | copy-start | bytes 1179652
  2.0 33.0 %copy-start.1 = (f32[3,4,64,128]{3,2,1,0:T(8,128)S(1)}, f32[3,4,64,128]{3,2,1,0:T(8,128)}, u32[]{:S(2)}) copy-start(f32[3,4,64,128]{3,2,1,0:T(8,128)} %w.3) | copy-start | bytes 1179652
  2.0 33.0 %copy-start.3 = (f32[3,4,64,128]{3,2,1,0:T(8,128)S(1)}, f32[3,4,64,128]{3,2,1,0:T(8,128)}, u32[]{:S(2)}) copy-start(f32[3,4,64,128]{3,2,1,0:T(8,128)} %u.3) | copy-start | bytes 1179652
  3.9 31.0 %collective-permute-start = (f32[9,64,128]{2,1,0:T(8,128)S(1)}, f32[9,64,128]{2,1,0:T(8,128)S(1)}, u32[]{:S(2)}, u32[]{:S(2)}) collective-permute-start(f32[9,64,128]{2,1,0:T(8,128)S(1)} %get-tuple-element.20), channel_id=1, source_target_pairs={{0,8},{8,16},{16,24},{24,32},{32,40},{40,48},{48,56},{56,64},{64,7... | collective-permute-start | bytes 884744 | tf_op jit(solution)/shard_map/ppermute | solution.py:315
  6.0 28.9 %collective-permute-start.1 = (f32[9,64,128]{2,1,0:T(8,128)S(1)}, f32[9,64,128]{2,1,0:T(8,128)S(1)}, u32[]{:S(2)}, u32[]{:S(2)}) collective-permute-start(f32[9,64,128]{2,1,0:T(8,128)S(1)} %get-tuple-element.21), channel_id=1, source_target_pairs={{0,248},{8,0},{16,8},{24,16},{32,24},{40,32},{48,40},{56,48},{64,5... | collective-permute-start | bytes 884744 | tf_op jit(solution)/shard_map/ppermute | solution.py:316
  12.8 22.2 %all-to-all-start = ((f32[256,1,128]{2,1,0:T(1,128)}), f32[256,1,128]{2,1,0:T(1,128)S(1)}, u32[]{:S(2)}, u32[]{:S(2)}) async-start(f32[256,1,128]{2,1,0:T(1,128)} %bitcast.1), calls=%async_computation | async-start | bytes 262144 | tf_op jit(solution)/shard_map/all_to_all | solution.py:323
  22.3 7.5 %collective-permute-start.4 = (f32[2,9,4,128]{3,2,1,0:T(4,128)S(1)}, f32[2,9,4,128]{3,2,1,0:T(4,128)S(1)}, u32[]{:S(2)}, u32[]{:S(2)}) collective-permute-start(f32[2,9,4,128]{3,2,1,0:T(4,128)S(1)} %get-tuple-element.24), channel_id=1, source_target_pairs={{0,1},{1,0},{2,3},{3,2},{4,5},{5,4},{6,7},{7,6},{8,9},{9,8},{10,11... | collective-permute-start | bytes 110600 | tf_op jit(solution)/shard_map/ppermute | solution.py:319
  25.2 2.0 %collective-permute-start.2 = (f32[64,128]{1,0:T(8,128)S(1)}, f32[64,128]{1,0:T(8,128)S(1)}, u32[]{:S(2)}, u32[]{:S(2)}) collective-permute-start(f32[64,128]{1,0:T(8,128)S(1)} %get-tuple-element.22), channel_id=1, source_target_pairs={{0,2},{2,4},{4,6},{6,0},{1,3},{3,5},{5,7},{7,1},{8,10},{10,12},{12... | collective-permute-start | bytes 98312 | tf_op jit(solution)/shard_map/ppermute | solution.py:317
  26.1 3.7 %collective-permute-start.3 = (f32[64,128]{1,0:T(8,128)S(1)}, f32[64,128]{1,0:T(8,128)S(1)}, u32[]{:S(2)}, u32[]{:S(2)}) collective-permute-start(f32[64,128]{1,0:T(8,128)S(1)} %get-tuple-element.23), channel_id=1, source_target_pairs={{0,6},{2,0},{4,2},{6,4},{1,7},{3,1},{5,3},{7,5},{8,14},{10,8},{12,... | collective-permute-start | bytes 98312 | tf_op jit(solution)/shard_map/ppermute | solution.py:318
  42.1 0.6 copy-start.4
  42.7 24.1 %collective-permute-start.5 = (f32[9,64,128]{2,1,0:T(8,128)}, f32[9,64,128]{2,1,0:T(8,128)S(1)}, u32[]{:S(2)}, u32[]{:S(2)}) collective-permute-start(f32[9,64,128]{2,1,0:T(8,128)} %get-tuple-element.28), channel_id=1, source_target_pairs={{0,8},{8,16},{16,24},{24,32},{32,40},{40,48},{48,56},{56,64},{64,7... | collective-permute-start | bytes 884744 | tf_op jit(solution)/shard_map/ppermute | solution.py:315
  43.0 23.7 %collective-permute-start.6 = (f32[9,64,128]{2,1,0:T(8,128)S(1)}, f32[9,64,128]{2,1,0:T(8,128)S(1)}, u32[]{:S(2)}, u32[]{:S(2)}) collective-permute-start(f32[9,64,128]{2,1,0:T(8,128)S(1)} %get-tuple-element.29), channel_id=1, source_target_pairs={{0,248},{8,0},{16,8},{24,16},{32,24},{40,32},{48,40},{56,48},{64,5... | collective-permute-start | bytes 884744 | tf_op jit(solution)/shard_map/ppermute | solution.py:316
  47.4 9.4 %copy-start.5 = (f32[64,128]{1,0:T(8,128)S(1)}, f32[64,128]{1,0:T(8,128)}, u32[]{:S(2)}) copy-start(f32[64,128]{1,0:T(8,128)} %copy-done.4) | copy-start | bytes 98308
  47.4 19.3 %all-to-all-start.1 = ((f32[256,1,128]{2,1,0:T(1,128)}), f32[256,1,128]{2,1,0:T(1,128)S(1)}, u32[]{:S(2)}, u32[]{:S(2)}) async-start(f32[256,1,128]{2,1,0:T(1,128)} %bitcast.4), calls=%async_computation.1 | async-start | bytes 262144 | tf_op jit(solution)/shard_map/all_to_all | solution.py:323
  53.9 7.6 %collective-permute-start.9 = (f32[2,9,4,128]{3,2,1,0:T(4,128)S(1)}, f32[2,9,4,128]{3,2,1,0:T(4,128)S(1)}, u32[]{:S(2)}, u32[]{:S(2)}) collective-permute-start(f32[2,9,4,128]{3,2,1,0:T(4,128)S(1)} %get-tuple-element.32), channel_id=1, source_target_pairs={{0,1},{1,0},{2,3},{3,2},{4,5},{5,4},{6,7},{7,6},{8,9},{9,8},{10,11... | collective-permute-start | bytes 110600 | tf_op jit(solution)/shard_map/ppermute | solution.py:319
  56.9 2.0 %collective-permute-start.7 = (f32[64,128]{1,0:T(8,128)S(1)}, f32[64,128]{1,0:T(8,128)S(1)}, u32[]{:S(2)}, u32[]{:S(2)}) collective-permute-start(f32[64,128]{1,0:T(8,128)S(1)} %copy-done.5), channel_id=1, source_target_pairs={{0,2},{2,4},{4,6},{6,0},{1,3},{3,5},{5,7},{7,1},{8,10},{10,12},{12... | collective-permute-start | bytes 98312 | tf_op jit(solution)/shard_map/ppermute | solution.py:317
  57.7 3.8 %collective-permute-start.8 = (f32[64,128]{1,0:T(8,128)S(1)}, f32[64,128]{1,0:T(8,128)S(1)}, u32[]{:S(2)}, u32[]{:S(2)}) collective-permute-start(f32[64,128]{1,0:T(8,128)S(1)} %get-tuple-element.31), channel_id=1, source_target_pairs={{0,6},{2,0},{4,2},{6,4},{1,7},{3,1},{5,3},{7,5},{8,14},{10,8},{12,... | collective-permute-start | bytes 98312 | tf_op jit(solution)/shard_map/ppermute | solution.py:318

commit v2 on v1

v2 whole, which is shorter than its diff:
```python
import numpy as np
import jax
import jax.numpy as jnp
from jax import lax
from jax.experimental import pallas as pl
from jax.experimental.pallas import tpu as pltpu
from jax.sharding import PartitionSpec as P


ENTRY_LIMIT = 53 * 1024 * 1024
COURANT = 0.4
SPEED_TOTAL = 1.72
SPEED_X, SPEED_Z, SPEED_Y = 0.6, 0.64, 0.48
ROWS = 8


def root_table(degree):
    points = np.cos((np.arange(400) + 0.5) * np.pi / 400)
    values = np.cos(2.0 / 3.0 * np.arccos(0.5 * (points + 1.0)))
    fit = np.polynomial.chebyshev.Chebyshev.fit(points, values, degree, domain=[-1, 1])
    return [float(c) for c in fit.convert(kind=np.polynomial.Polynomial).coef]


ROOT = root_table(11)


def cos_third(ratio):
    half = jnp.sqrt(jnp.maximum(0.5 + 0.5 * ratio, 0.0))
    t = 2.0 * half - 1.0
    total = jnp.full_like(t, ROOT[-1])
    for c in ROOT[-2::-1]:
        total = total * t + c
    return total


def limited(a, b):
    return jnp.maximum(jnp.minimum(a, b), 0.0) + jnp.minimum(jnp.maximum(a, b), 0.0)


def side_terms(c, wm2, wm1, w, wp1, wp2, um1, u, up1):
    d0, d1, d2, d3 = wm1 - wm2, w - wm1, wp1 - w, wp2 - wp1
    below = limited(d0, d1)
    here = (0.5 * c) * limited(d1, d2)
    above = limited(d2, d3)
    base = c * w
    own = (base + here) * jnp.maximum(u, 0.0) - (base - here) * jnp.minimum(u, 0.0)
    low = (wm1 + 0.5 * below) * (c * jnp.minimum(-um1, 0.0))
    high = (wp1 - 0.5 * above) * (c * jnp.minimum(up1, 0.0))
    return own, low, high


def odd_along(axis):
    return lax.rem(lax.axis_index(axis), 2)


def plane_at(x, odd):
    return x + odd * (3 - 2 * x)


class Nodes:
    def __init__(self, a, b, inner):
        self.a, self.b, self.inner = a, b, inner

    def w(self, n, x):
        return (self.a if x >= 2 else self.b).at[n if x in (0, 3) else 6 + n]

    def u(self, n, x):
        if x in (0, 3):
            return (self.a if x == 3 else self.b).at[3 + n]
        return self.inner.at[n if x == 2 else 3 + n]


class Fields(Nodes):
    def __init__(self, a, b, inner, xa, xb, ya, yb, pw, pu):
        super().__init__(a, b, inner)
        self.xa, self.xb, self.ya, self.yb, self.pw, self.pu = xa, xb, ya, yb, pw, pu
        self.sign = 1.0 - 2.0 * odd_along("gx").astype(jnp.float32)
        self.y_odd = odd_along("gy")

    def plane_w(self, n, x):
        if x in (-1, 4):
            return (self.xa if x == 4 else self.xb).at[n]
        if x in (-2, 5):
            return (self.xa if x == 5 else self.xb).at[6 + n]
        return self.w(n, x)

    def plane_u(self, n, x):
        if x in (-1, 4):
            return (self.xa if x == 4 else self.xb).at[3 + n]
        return self.u(n, x)


def pad_rows(f, zr):
    def copy(i, carry):
        z = pl.ds(pl.multiple_of(i * ROWS, ROWS), ROWS)
        zp = pl.ds(pl.multiple_of(i * ROWS + 8, ROWS), ROWS)
        for n in range(3):
            for x in range(4):
                f.pw[n, x, zp, :] = f.w(n, x)[z, :]
                f.pu[n, x, zp, :] = f.u(n, x)[z, :]
        return carry

    lax.fori_loop(0, 64 // ROWS, copy, 0)
    f.pw[:, :, 7, :] = zr[0, 0:3]
    f.pu[:, :, 7, :] = zr[0, 3:6]
    f.pw[:, :, 6, :] = zr[0, 6:9]
    f.pw[:, :, 72, :] = zr[1, 0:3]
    f.pu[:, :, 72, :] = zr[1, 3:6]
    f.pw[:, :, 73, :] = zr[1, 6:9]


def divergence(f, i, x, lane):
    z0 = i * ROWS
    z = pl.ds(pl.multiple_of(z0, ROWS), ROWS)
    first, final = lane == 0, lane == 127
    flip = f.y_odd == 1
    ha, hb = f.ya[z, :], f.yb[z, :]
    hlo, hhi = jnp.where(flip, ha, hb), jnp.where(flip, hb, ha)

    def halo_lo(k):
        return pltpu.roll(hlo, (128 - (4 * k + x)) % 128, 1)

    def halo_hi(k):
        return pltpu.roll(hhi, 127 - (4 * k + x), 1)

    total = [None] * 6
    for n in range(3):
        w, u = f.w(n, x)[z, :], f.u(n, x)[z, :]
        parts = []
        um1, up1 = f.plane_u(n, x - 1)[z, :], f.plane_u(n, x + 1)[z, :]
        own, low, high = side_terms(
            SPEED_X, *[f.plane_w(n, x + s)[z, :] for s in (-2, -1)], w,
            *[f.plane_w(n, x + s)[z, :] for s in (1, 2)], f.sign * um1, f.sign * u, f.sign * up1)
        parts += [(low, um1), (high, up1)]

        def row_w(s):
            return f.pw[n, x, pl.ds(z0 + 8 + s, ROWS), :]

        um1, up1 = f.pu[n, x, pl.ds(z0 + 7, ROWS), :], f.pu[n, x, pl.ds(z0 + 9, ROWS), :]
        own_z, low, high = side_terms(
            SPEED_Z, row_w(-2), row_w(-1), w, row_w(1), row_w(2), um1, u, up1)
        parts += [(low, um1), (high, up1)]
        own = own + own_z
        um1 = jnp.where(first, halo_lo(3 + n), pltpu.roll(u, 1, 1))
        up1 = jnp.where(final, halo_hi(3 + n), pltpu.roll(u, 127, 1))
        wm1 = jnp.where(first, halo_lo(n), pltpu.roll(w, 1, 1))
        wp1 = jnp.where(final, halo_hi(n), pltpu.roll(w, 127, 1))
        wm2 = jnp.where(first, halo_lo(6 + n), pltpu.roll(wm1, 1, 1))
        wp2 = jnp.where(final, halo_hi(6 + n), pltpu.roll(wp1, 127, 1))
        own_y, low, high = side_terms(SPEED_Y, wm2, wm1, w, wp1, wp2, um1, u, up1)
        parts += [(low, um1), (high, up1)]
        own = own + own_y
        parts.append((own, u))
        for order in range(6):
            term = parts[0][0]
            for value, _ in parts[1:]:
                term = term + value
            total[order] = term if total[order] is None else total[order] + term
            if order < 5:
                parts = [(value * speed, speed) for value, speed in parts]
    return total


def moments_of(nodes):
    total = [None] * 6
    for w, u in nodes:
        power = w
        for order in range(6):
            total[order] = power if total[order] is None else total[order] + power
            if order < 5:
                power = power * u
    return total


def invert(mom):
    inv0 = 1.0 / mom[0]
    a0 = mom[1] * inv0
    s1 = [None] + [mom[l + 1] - a0 * mom[l] for l in range(1, 5)]
    inv1 = 1.0 / s1[1]
    quot = s1[2] * inv1
    a1 = quot - a0
    b1 = s1[1] * inv0
    s2_two = s1[3] - a1 * s1[2] - b1 * mom[2]
    s2_three = s1[4] - a1 * s1[3] - b1 * mom[3]
    a2 = s2_three / s2_two - quot
    b2 = s2_two * inv1
    q = (a0 + a1 + a2) * (1.0 / 3.0)
    d0, d1, d2 = a0 - q, a1 - q, a2 - q
    square = (d0 * d0 + d1 * d1 + d2 * d2 + 2.0 * b1 + 2.0 * b2) * (1.0 / 6.0)
    p = jnp.sqrt(square)
    det = d0 * d1 * d2 - d0 * b2 - d2 * b1
    ratio = det / (2.0 * square * p)
    high = q + 2.0 * p * cos_third(ratio)
    low = q - 2.0 * p * cos_third(-ratio)
    middle = 3.0 * q - high - low
    both = b1 * b2
    scale = mom[0] * both
    nodes = []
    for value in (low, middle, high):
        e0 = value - a0
        e1 = (value - a1) * e0 - b1
        nodes.append((scale / (both + b2 * (e0 * e0) + e1 * e1), value))
    return nodes


def lanes():
    return lax.broadcasted_iota(jnp.int32, (ROWS, 128), 1)


def rows_of(i):
    return pl.ds(pl.multiple_of(i * ROWS, ROWS), ROWS)


def write_top(top, mx):
    mx[...] = jnp.full(mx.shape, jnp.max(top), jnp.float32)


def step_of(received):
    top = jnp.max(received[...], axis=0, keepdims=True)
    return COURANT / (SPEED_TOTAL * top)


def relay_kernel(got, mx):
    mx[...] = jnp.broadcast_to(jnp.max(got[...], axis=0, keepdims=True), mx.shape)


def entry_kernel(w, u, a, b, inner, mx, sems):
    nodes = Nodes(a, b, inner)
    odd = odd_along("gx")
    loads = [
        pltpu.make_async_copy(array.at[n, plane_at(x, odd)], side(n, x), sems.at[at, n, x])
        for at, (array, side) in enumerate(((u, nodes.u), (w, nodes.w)))
        for n in range(3) for x in range(4)
    ]
    for copy in loads:
        copy.start()
    top = jnp.zeros((ROWS, 128), jnp.float32)
    for at in range(12):
        loads[at].wait()
        for i in range(64 // ROWS):
            top = jnp.maximum(top, jnp.abs(nodes.u(at // 4, at % 4)[i * ROWS:(i + 1) * ROWS, :]))
    write_top(top, mx)
    for copy in loads[12:]:
        copy.wait()


def edge_kernel(a, b, inner, ya, yb, zs):
    nodes = Nodes(a, b, inner)
    lane = lanes()
    flip = odd_along("gy") == 1
    for n in range(3):
        for x in range(4):
            w, u = nodes.w(n, x), nodes.u(n, x)
            for k, row, other, side in ((n, 63, 0, w), (3 + n, 63, 0, u), (6 + n, 62, 1, w)):
                zs[0, k, x, :] = side[row, :]
                zs[1, k, x, :] = side[other, :]

    def rows(i, carry):
        z = rows_of(i)
        up = jnp.zeros((ROWS, 128), jnp.float32)
        dn = up
        for n in range(3):
            for x in range(4):
                vw, vu = nodes.w(n, x)[z, :], nodes.u(n, x)[z, :]
                for k, value, ahead, back in ((n, vw, 127, 0), (3 + n, vu, 127, 0), (6 + n, vw, 126, 1)):
                    at = 4 * k + x
                    up = jnp.where(lane == at, pltpu.roll(value, (at - ahead) % 128, 1), up)
                    dn = jnp.where(lane == at, pltpu.roll(value, (at - back) % 128, 1), dn)
        ya[z, :] = jnp.where(flip, dn, up)
        yb[z, :] = jnp.where(flip, up, dn)
        return carry

    lax.fori_loop(0, 64 // ROWS, rows, 0)


def change_kernel(a, b, inner, xa, xb, ya, yb, zr, out, pw, pu):
    f = Fields(a, b, inner, xa, xb, ya, yb, pw, pu)
    pad_rows(f, zr)
    lane = lanes()

    def rows(i, carry):
        for x in range(4):
            for k, value in enumerate(divergence(f, i, x, lane)):
                out[k, x, rows_of(i), :] = value
        return carry

    lax.fori_loop(0, 64 // ROWS, rows, 0)


def middle_kernel(change, a, b, inner, got, base, mid_a, mid_b, mid_inner, mx):
    step = step_of(got)
    old, new = Nodes(a, b, inner), Nodes(mid_a, mid_b, mid_inner)

    def rows(i, top):
        z = rows_of(i)
        for x in range(4):
            mid = []
            for k, moment in enumerate(moments_of([(old.w(n, x)[z, :], old.u(n, x)[z, :]) for n in range(3)])):
                mid.append(moment - step * change[k, x, z, :])
                base[k, x, z, :] = 0.5 * (moment + mid[k])
            for n, (weight, speed) in enumerate(invert(mid)):
                new.w(n, x)[z, :] = weight
                new.u(n, x)[z, :] = speed
                top = jnp.maximum(top, jnp.abs(speed))
        return top

    top = lax.fori_loop(0, 64 // ROWS, rows, jnp.zeros((ROWS, 128), jnp.float32))
    write_top(top, mx)


def exit_kernel(change, base, got, out, held, sems):
    half = 0.5 * step_of(got)
    odd = odd_along("gx")
    stores = []
    for k in range(6):
        for x in range(4):
            held[k, x] = base[k, x] - half * change[k, x]
            stores.append(pltpu.make_async_copy(held.at[k, x], out.at[k, plane_at(x, odd)], sems.at[k, x]))
            stores[-1].start()
    for copy in stores:
        copy.wait()


def f32(*shape):
    return jax.ShapeDtypeStruct(shape, jnp.float32)


PLANES = (f32(9, 64, 128), f32(9, 64, 128), f32(6, 64, 128))
EDGES = (f32(64, 128), f32(64, 128), f32(2, 9, 4, 128))
MOMENTS = f32(6, 4, 64, 128)
PADDED = [pltpu.VMEM((3, 4, 80, 128), jnp.float32)] * 2
VM = pl.BlockSpec(memory_space=pltpu.VMEM)
ANY = pl.BlockSpec(memory_space=pltpu.HBM)


def call(kernel, outs, args, scratch=(), ins=VM, out=VM, flops=1, limit=8 * 1024 * 1024):
    return pl.pallas_call(
        kernel,
        out_shape=outs,
        in_specs=[ins] * len(args),
        out_specs=out if isinstance(out, tuple) else jax.tree.map(lambda _: out, outs),
        scratch_shapes=list(scratch),
        cost_estimate=pl.CostEstimate(flops=flops, bytes_accessed=1 << 20, transcendentals=0),
        compiler_params=pltpu.CompilerParams(vmem_limit_bytes=limit),
    )(*args)


def pairs(n, first):
    return [(i, (i + 1) % n) for i in range(first, n, 2)] + [((i + 1) % n, i) for i in range(first, n, 2)]


def local(weights, abscissas):
    nx, ny, nz = (lax.axis_size(a) for a in ("gx", "gy", "gz"))
    swap = [(i, (i + 1) % nz) for i in range(nz)]

    def exchange(xa, xb, ya, yb, zs):
        return (
            lax.ppermute(xa, "gx", pairs(nx, 0)),
            lax.ppermute(xb, "gx", pairs(nx, 1)),
            lax.ppermute(ya, "gy", pairs(ny, 0)),
            lax.ppermute(yb, "gy", pairs(ny, 1)),
            lax.ppermute(zs, "gz", swap),
        )

    def spread(top, axes, n):
        return lax.all_to_all(top.reshape(n, 1, 128), axes, 0, 0).reshape(n, 128)

    def largest(top):
        got = spread(top, ("gy", "gz"), ny * nz)
        top = call(relay_kernel, f32(nx, 128), (got,))
        return spread(top, ("gx",), nx)

    tops = f32(ny * nz, 128)
    *planes, top = call(
        entry_kernel, PLANES + (tops,), (weights, abscissas),
        [pltpu.SemaphoreType.DMA((2, 3, 4))], ins=ANY, limit=ENTRY_LIMIT)
    edges = call(edge_kernel, EDGES, planes, flops=2 << 20)
    halo = exchange(*planes[:2], *edges)
    got = largest(top)
    change = call(change_kernel, MOMENTS, (*planes, *halo), PADDED, flops=4 << 20)
    base, *planes, top = call(
        middle_kernel, (MOMENTS,) + PLANES + (tops,), (change, *planes, got), flops=4 << 20)
    edges = call(edge_kernel, EDGES, planes, flops=2 << 20)
    halo = exchange(*planes[:2], *edges)
    got = largest(top)
    change = call(change_kernel, MOMENTS, (*planes, *halo), PADDED, flops=4 << 20)
    return call(
        exit_kernel, MOMENTS, (change, base, got),
        [pltpu.VMEM((6, 4, 64, 128), jnp.float32), pltpu.SemaphoreType.DMA((6, 4))], out=ANY)


def solution(mesh):
    spec = P(None, "gx", "gz", "gy")
    return jax.shard_map(local, mesh=mesh, in_specs=(spec, spec), out_specs=spec, check_vma=False)
```

time: 71.2 us -> 70.6 us (level)
  local copies, waits for them, and re-layouts: 2.6 us -> 0 us
  Pallas kernels: 13.2 us -> 15.2 us
  waiting for transfers between devices: 17.9 us -> 15.9 us
  starting transfers between devices: 37.2 us -> 39 us
    ppermute x10, waiting for transfers between devices: 7.51 us -> 0.03 us  [the longest x2 0.01 us: exchange(): lax.ppermute(yb, 'gy', pairs(ny, 1))]
    all_to_all x2 -> x4, waiting for transfers between devices: 10.3 us -> 15.9 us  [spread(): return lax.all_to_all(top.reshape(n, 1, 128), axes, 0, 0).reshape(n, 128)]
    all_to_all x2 -> x4, starting transfers between devices: 15.9 us -> 21.1 us  [spread(): return lax.all_to_all(top.reshape(n, 1, 128), axes, 0, 0).reshape(n, 128)]
    ppermute x10, starting transfers between devices: 21.3 us -> 17.9 us  [the longest x2 8.09 us: exchange(): lax.ppermute(xb, 'gx', pairs(nx, 1))]
    unnamed x12 -> x0, local copies, waits for them, and re-layouts: 2.6 us -> none
    pallas_call x3 -> x9, Pallas kernels: 13.2 us -> 15.2 us  [call(): pl.pallas_call(kernel, out_shape=outs, in_specs=[ins] * len(args), out_sp...]
  transfers between devices with their start and end apart: 12 -> 14, of which waited for: 6 -> 4; matrix products, arithmetic and copies ran while one was open for 0% -> 0% of each run, Pallas kernels for 0% -> 14%
where the time goes in v2:
time: 70.6 us; the launch traced here: 70.2 us
  starting transfers between devices  39 us (55%)
  waiting for transfers between devices  15.9 us (23%)
  Pallas kernels  15.2 us (22%)
    all_to_all x4, starting transfers between devices, spread(): return lax.all_to_all(top.reshape(n, 1, 128), axes, 0, 0).reshape(n, 128)  21.1 us
    all_to_all x4, waiting for transfers between devices, spread(): return lax.all_to_all(top.reshape(n, 1, 128), axes, 0, 0).reshape(n, 128)  15.9 us
    pallas_call x9, Pallas kernels, call(): pl.pallas_call(kernel, out_shape=outs, in_specs=[ins] * len(args), out_sp...  15.2 us
    ppermute x2, starting transfers between devices, exchange(): lax.ppermute(xb, 'gx', pairs(nx, 1))  8.09 us
    ppermute x2, starting transfers between devices, exchange(): lax.ppermute(zs, 'gz', swap)  3.83 us
    ppermute x2, starting transfers between devices, exchange(): lax.ppermute(yb, 'gy', pairs(ny, 1))  3.33 us
    ppermute x2, starting transfers between devices, exchange(): lax.ppermute(xa, 'gx', pairs(nx, 0))  2.5 us
  transfers between devices with their start and end apart: 14, of which 4 were waited for; matrix products, arithmetic and copies ran while one was open for 0% of the time, Pallas kernels for 14%

profile of v2, /device:TPU:1, one launch (start us, length us, event | category | flops | bytes accessed | tf_op | source)
XLA Modules:
  0.0 70.2 jit_solution(3130629259600039276)
XLA Ops:
  0.0 1.9 %shard_map.28 = (f32[9,64,128]{2,1,0:T(8,128)S(1)}, f32[9,64,128]{2,1,0:T(8,128)S(1)}, f32[6,64,128]{2,1,0:T(8,128)S(1)}, f32[8,128]{1,0:T(8,128)}) custom-call(f32[3,4,64,128]{3,2,1,0:T(8,128)} %w.1, f32[3,4,64,128]{3,2,1,0:T(8,128)} %u.1), custom_call_target="tpu_custom_call" | custom-call | flops 1 | bytes 1048576 | tf_op jit(solution)/shard_map/pallas_call | solution.py:337
  1.9 2.2 %collective-permute-start = (f32[9,64,128]{2,1,0:T(8,128)S(1)}, f32[9,64,128]{2,1,0:T(8,128)S(1)}, u32[]{:S(2)}, u32[]{:S(2)}) collective-permute-start(f32[9,64,128]{2,1,0:T(8,128)S(1)} %get-tuple-element.20.a), channel_id=1, source_target_pairs={{0,8},{16,24},{32,40},{48,56},{64,72},{80,88},{96,104},{112,120},{... | collective-permute-start | bytes 884744 | tf_op jit(solution)/shard_map/ppermute | solution.py:358
  4.1 7.2 %collective-permute-start.1 = (f32[9,64,128]{2,1,0:T(8,128)S(1)}, f32[9,64,128]{2,1,0:T(8,128)S(1)}, u32[]{:S(2)}, u32[]{:S(2)}) collective-permute-start(f32[9,64,128]{2,1,0:T(8,128)S(1)} %get-tuple-element.21.b), channel_id=1, source_target_pairs={{8,16},{24,32},{40,48},{56,64},{72,80},{88,96},{104,112},{120,128}... | collective-permute-start | bytes 884744 | tf_op jit(solution)/shard_map/ppermute | solution.py:359
  11.3 1.2 %shard_map.29 = (f32[64,128]{1,0:T(8,128)S(1)}, f32[64,128]{1,0:T(8,128)S(1)}, f32[2,9,4,128]{3,2,1,0:T(4,128)S(1)}) custom-call(f32[9,64,128]{2,1,0:T(8,128)S(1)} %get-tuple-element.20.a, f32[9,64,128]{2,1,0:T(8,128)S(1)} %get-tuple-element.21.b, f32[6,64,128]{2,1,0:T(8,128)S(1)} %get-tuple-element.22.inner), custom_call_target="tpu_custom_call" | custom-call | flops 2097152 | bytes 1048576 | tf_op jit(solution)/shard_map/pallas_call | solution.py:337
  12.5 2.8 %collective-permute-start.4 = (f32[2,9,4,128]{3,2,1,0:T(4,128)S(1)}, f32[2,9,4,128]{3,2,1,0:T(4,128)S(1)}, u32[]{:S(2)}, u32[]{:S(2)}) collective-permute-start(f32[2,9,4,128]{3,2,1,0:T(4,128)S(1)} %get-tuple-element.25), channel_id=1, source_target_pairs={{0,1},{1,0},{2,3},{3,2},{4,5},{5,4},{6,7},{7,6},{8,9},{9,8},{10,11... | collective-permute-start | bytes 110600 | tf_op jit(solution)/shard_map/ppermute | solution.py:362
  15.3 4.7 %all-to-all-start = ((f32[8,1,128]{2,1,0:T(1,128)}), f32[8,1,128]{2,1,0:T(1,128)S(1)}, u32[]{:S(2)}, u32[]{:S(2)}) async-start(f32[8,1,128]{2,1,0:T(1,128)} %bitcast.1), calls=%async_computation | async-start | bytes 8192 | tf_op jit(solution)/shard_map/all_to_all | solution.py:366
  20.2 1.6 %collective-permute-start.3 = (f32[64,128]{1,0:T(8,128)S(1)}, f32[64,128]{1,0:T(8,128)S(1)}, u32[]{:S(2)}, u32[]{:S(2)}) collective-permute-start(f32[64,128]{1,0:T(8,128)S(1)} %get-tuple-element.24), channel_id=1, source_target_pairs={{2,4},{6,0},{4,2},{0,6},{3,5},{7,1},{5,3},{1,7},{10,12},{14,8},{12... | collective-permute-start | bytes 98312 | tf_op jit(solution)/shard_map/ppermute | solution.py:361
  21.8 2.7 %all-to-all-done = f32[8,1,128]{2,1,0:T(1,128)S(1)} async-done(((f32[8,1,128]{2,1,0:T(1,128)}), f32[8,1,128]{2,1,0:T(1,128)S(1)}, u32[]{:S(2)}, u32[]{:S(2)}) %all-to-all-start) | async-done | bytes 4128 | tf_op jit(solution)/shard_map/all_to_all | solution.py:366
  24.6 0.6 shard_map.31
  25.2 4.2 %all-to-all-start.1 = ((f32[32,1,128]{2,1,0:T(1,128)}), f32[32,1,128]{2,1,0:T(1,128)S(1)}, u32[]{:S(2)}, u32[]{:S(2)}) async-start(f32[32,1,128]{2,1,0:T(1,128)} %bitcast.4), calls=%async_computation.1 | async-start | bytes 32768 | tf_op jit(solution)/shard_map/all_to_all | solution.py:366
  29.5 3.3 %shard_map.30.change = f32[6,4,64,128]{3,2,1,0:T(8,128)S(1)} custom-call(f32[9,64,128]{2,1,0:T(8,128)S(1)} %get-tuple-element.20.a, f32[9,64,128]{2,1,0:T(8,128)S(1)} %get-tuple-element.21.b, f32[6,64,128]{2,1,0:T(8,128)S(1)} %get-tuple-element.22.inner, f32[9,64,128]{2,1,0:T(8,128)S(1)} %collective-permute-done.xa, ...), custom_call_target="tpu_custom_call" | custom-call | flops 4194304 | bytes 1048576 | tf_op jit(solution)/shard_map/pallas_call | solution.py:337
  32.8 5.2 %all-to-all-done.1 = f32[32,1,128]{2,1,0:T(1,128)S(1)} async-done(((f32[32,1,128]{2,1,0:T(1,128)}), f32[32,1,128]{2,1,0:T(1,128)S(1)}, u32[]{:S(2)}, u32[]{:S(2)}) %all-to-all-start.1) | async-done | bytes 16416 | tf_op jit(solution)/shard_map/all_to_all | solution.py:366
  37.9 2.0 %shard_map.32 = (f32[6,4,64,128]{3,2,1,0:T(8,128)S(1)}, f32[9,64,128]{2,1,0:T(8,128)S(1)}, f32[9,64,128]{2,1,0:T(8,128)S(1)}, f32[6,64,128]{2,1,0:T(8,128)S(1)}, f32[8,128]{1,0:T(8,128)}) custom-call(f32[6,4,64,128]{3,2,1,0:T(8,128)S(1)} %shard_map.30.change, f32[9,64,128]{2,1,0:T(8,128)S(1)} %get-tuple-element.20.a, f32[9,64,128]{2,1,0:T(8,128)S(1)} %get-tuple-element.21.b, ...), custom_call_target="tpu_custom_call" | custom-call | flops 4194304 | bytes 1048576 | tf_op jit(solution)/shard_map/pallas_call | solution.py:337
  40.3 0.9 %collective-permute-start.6 = (f32[9,64,128]{2,1,0:T(8,128)S(1)}, f32[9,64,128]{2,1,0:T(8,128)S(1)}, u32[]{:S(2)}, u32[]{:S(2)}) collective-permute-start(f32[9,64,128]{2,1,0:T(8,128)S(1)} %get-tuple-element.28.b), channel_id=1, source_target_pairs={{8,16},{24,32},{40,48},{56,64},{72,80},{88,96},{104,112},{120,128}... | collective-permute-start | bytes 884744 | tf_op jit(solution)/shard_map/ppermute | solution.py:359
  41.2 1.2 %shard_map.33 = (f32[64,128]{1,0:T(8,128)S(1)}, f32[64,128]{1,0:T(8,128)S(1)}, f32[2,9,4,128]{3,2,1,0:T(4,128)S(1)}) custom-call(f32[9,64,128]{2,1,0:T(8,128)S(1)} %get-tuple-element.27.a, f32[9,64,128]{2,1,0:T(8,128)S(1)} %get-tuple-element.28.b, f32[6,64,128]{2,1,0:T(8,128)S(1)} %get-tuple-element.29.inner), custom_call_target="tpu_custom_call" | custom-call | flops 2097152 | bytes 1048576 | tf_op jit(solution)/shard_map/pallas_call | solution.py:337
  42.4 1.0 %collective-permute-start.9 = (f32[2,9,4,128]{3,2,1,0:T(4,128)S(1)}, f32[2,9,4,128]{3,2,1,0:T(4,128)S(1)}, u32[]{:S(2)}, u32[]{:S(2)}) collective-permute-start(f32[2,9,4,128]{3,2,1,0:T(4,128)S(1)} %get-tuple-element.32), channel_id=1, source_target_pairs={{0,1},{1,0},{2,3},{3,2},{4,5},{5,4},{6,7},{7,6},{8,9},{9,8},{10,11... | collective-permute-start | bytes 110600 | tf_op jit(solution)/shard_map/ppermute | solution.py:362
  43.4 6.6 %all-to-all-start.2 = ((f32[8,1,128]{2,1,0:T(1,128)}), f32[8,1,128]{2,1,0:T(1,128)S(1)}, u32[]{:S(2)}, u32[]{:S(2)}) async-start(f32[8,1,128]{2,1,0:T(1,128)} %bitcast.7), calls=%async_computation.2 | async-start | bytes 8192 | tf_op jit(solution)/shard_map/all_to_all | solution.py:366
  49.9 1.7 %collective-permute-start.8 = (f32[64,128]{1,0:T(8,128)S(1)}, f32[64,128]{1,0:T(8,128)S(1)}, u32[]{:S(2)}, u32[]{:S(2)}) collective-permute-start(f32[64,128]{1,0:T(8,128)S(1)} %get-tuple-element.31), channel_id=1, source_target_pairs={{2,4},{6,0},{4,2},{0,6},{3,5},{7,1},{5,3},{1,7},{10,12},{14,8},{12... | collective-permute-start | bytes 98312 | tf_op jit(solution)/shard_map/ppermute | solution.py:361
  51.7 2.8 %all-to-all-done.2 = f32[8,1,128]{2,1,0:T(1,128)S(1)} async-done(((f32[8,1,128]{2,1,0:T(1,128)}), f32[8,1,128]{2,1,0:T(1,128)S(1)}, u32[]{:S(2)}, u32[]{:S(2)}) %all-to-all-start.2) | async-done | bytes 4128 | tf_op jit(solution)/shard_map/all_to_all | solution.py:366
  54.4 0.6 shard_map.35
  55.1 5.5 %all-to-all-start.3 = ((f32[32,1,128]{2,1,0:T(1,128)}), f32[32,1,128]{2,1,0:T(1,128)S(1)}, u32[]{:S(2)}, u32[]{:S(2)}) async-start(f32[32,1,128]{2,1,0:T(1,128)} %bitcast.10), calls=%async_computation.3 | async-start | bytes 32768 | tf_op jit(solution)/shard_map/all_to_all | solution.py:366
  60.7 3.3 %shard_map.34.change = f32[6,4,64,128]{3,2,1,0:T(8,128)S(1)} custom-call(f32[9,64,128]{2,1,0:T(8,128)S(1)} %get-tuple-element.27.a, f32[9,64,128]{2,1,0:T(8,128)S(1)} %get-tuple-element.28.b, f32[6,64,128]{2,1,0:T(8,128)S(1)} %get-tuple-element.29.inner, f32[9,64,128]{2,1,0:T(8,128)S(1)} %collective-permute-done.5.xa, ...), custom_call_target="tpu_custom_call" | custom-call | flops 4194304 | bytes 1048576 | tf_op jit(solution)/shard_map/pallas_call | solution.py:337
  64.0 5.2 %all-to-all-done.3 = f32[32,1,128]{2,1,0:T(1,128)S(1)} async-done(((f32[32,1,128]{2,1,0:T(1,128)}), f32[32,1,128]{2,1,0:T(1,128)S(1)}, u32[]{:S(2)}, u32[]{:S(2)}) %all-to-all-start.3) | async-done | bytes 16416 | tf_op jit(solution)/shard_map/all_to_all | solution.py:366
  69.1 1.1 %shard_map.36 = f32[6,4,64,128]{3,2,1,0:T(8,128)} custom-call(f32[6,4,64,128]{3,2,1,0:T(8,128)S(1)} %shard_map.34.change, f32[6,4,64,128]{3,2,1,0:T(8,128)S(1)} %get-tuple-element.33.base, f32[32,128]{1,0:T(8,128)S(1)} %bitcast.17), custom_call_target="tpu_custom_call" | custom-call | flops 1 | bytes 1048576 | tf_op jit(solution)/shard_map/pallas_call | solution.py:337
  (13 shorter events, 0.5 us)
Async XLA Ops:
  1.9 27.6 %collective-permute-start = (f32[9,64,128]{2,1,0:T(8,128)S(1)}, f32[9,64,128]{2,1,0:T(8,128)S(1)}, u32[]{:S(2)}, u32[]{:S(2)}) collective-permute-start(f32[9,64,128]{2,1,0:T(8,128)S(1)} %get-tuple-element.20.a), channel_id=1, source_target_pairs={{0,8},{16,24},{32,40},{48,56},{64,72},{80,88},{96,104},{112,120},{... | collective-permute-start | bytes 884744 | tf_op jit(solution)/shard_map/ppermute | solution.py:358
  4.1 25.4 %collective-permute-start.1 = (f32[9,64,128]{2,1,0:T(8,128)S(1)}, f32[9,64,128]{2,1,0:T(8,128)S(1)}, u32[]{:S(2)}, u32[]{:S(2)}) collective-permute-start(f32[9,64,128]{2,1,0:T(8,128)S(1)} %get-tuple-element.21.b), channel_id=1, source_target_pairs={{8,16},{24,32},{40,48},{56,64},{72,80},{88,96},{104,112},{120,128}... | collective-permute-start | bytes 884744 | tf_op jit(solution)/shard_map/ppermute | solution.py:359
  12.5 17.0 %collective-permute-start.4 = (f32[2,9,4,128]{3,2,1,0:T(4,128)S(1)}, f32[2,9,4,128]{3,2,1,0:T(4,128)S(1)}, u32[]{:S(2)}, u32[]{:S(2)}) collective-permute-start(f32[2,9,4,128]{3,2,1,0:T(4,128)S(1)} %get-tuple-element.25), channel_id=1, source_target_pairs={{0,1},{1,0},{2,3},{3,2},{4,5},{5,4},{6,7},{7,6},{8,9},{9,8},{10,11... | collective-permute-start | bytes 110600 | tf_op jit(solution)/shard_map/ppermute | solution.py:362
  15.3 9.3 %all-to-all-start = ((f32[8,1,128]{2,1,0:T(1,128)}), f32[8,1,128]{2,1,0:T(1,128)S(1)}, u32[]{:S(2)}, u32[]{:S(2)}) async-start(f32[8,1,128]{2,1,0:T(1,128)} %bitcast.1), calls=%async_computation | async-start | bytes 8192 | tf_op jit(solution)/shard_map/all_to_all | solution.py:366
  20.0 9.4 %collective-permute-start.2 = (f32[64,128]{1,0:T(8,128)S(1)}, f32[64,128]{1,0:T(8,128)S(1)}, u32[]{:S(2)}, u32[]{:S(2)}) collective-permute-start(f32[64,128]{1,0:T(8,128)S(1)} %get-tuple-element.23), channel_id=1, source_target_pairs={{0,2},{4,6},{2,0},{6,4},{1,3},{5,7},{3,1},{7,5},{8,10},{12,14},{10... | collective-permute-start | bytes 98312 | tf_op jit(solution)/shard_map/ppermute | solution.py:360
  20.2 9.2 %collective-permute-start.3 = (f32[64,128]{1,0:T(8,128)S(1)}, f32[64,128]{1,0:T(8,128)S(1)}, u32[]{:S(2)}, u32[]{:S(2)}) collective-permute-start(f32[64,128]{1,0:T(8,128)S(1)} %get-tuple-element.24), channel_id=1, source_target_pairs={{2,4},{6,0},{4,2},{0,6},{3,5},{7,1},{5,3},{1,7},{10,12},{14,8},{12... | collective-permute-start | bytes 98312 | tf_op jit(solution)/shard_map/ppermute | solution.py:361
  25.2 12.8 %all-to-all-start.1 = ((f32[32,1,128]{2,1,0:T(1,128)}), f32[32,1,128]{2,1,0:T(1,128)S(1)}, u32[]{:S(2)}, u32[]{:S(2)}) async-start(f32[32,1,128]{2,1,0:T(1,128)} %bitcast.4), calls=%async_computation.1 | async-start | bytes 32768 | tf_op jit(solution)/shard_map/all_to_all | solution.py:366
  40.0 20.7 %collective-permute-start.5 = (f32[9,64,128]{2,1,0:T(8,128)S(1)}, f32[9,64,128]{2,1,0:T(8,128)S(1)}, u32[]{:S(2)}, u32[]{:S(2)}) collective-permute-start(f32[9,64,128]{2,1,0:T(8,128)S(1)} %get-tuple-element.27.a), channel_id=1, source_target_pairs={{0,8},{16,24},{32,40},{48,56},{64,72},{80,88},{96,104},{112,120},{... | collective-permute-start | bytes 884744 | tf_op jit(solution)/shard_map/ppermute | solution.py:358
  40.3 20.4 %collective-permute-start.6 = (f32[9,64,128]{2,1,0:T(8,128)S(1)}, f32[9,64,128]{2,1,0:T(8,128)S(1)}, u32[]{:S(2)}, u32[]{:S(2)}) collective-permute-start(f32[9,64,128]{2,1,0:T(8,128)S(1)} %get-tuple-element.28.b), channel_id=1, source_target_pairs={{8,16},{24,32},{40,48},{56,64},{72,80},{88,96},{104,112},{120,128}... | collective-permute-start | bytes 884744 | tf_op jit(solution)/shard_map/ppermute | solution.py:359
  42.4 18.3 %collective-permute-start.9 = (f32[2,9,4,128]{3,2,1,0:T(4,128)S(1)}, f32[2,9,4,128]{3,2,1,0:T(4,128)S(1)}, u32[]{:S(2)}, u32[]{:S(2)}) collective-permute-start(f32[2,9,4,128]{3,2,1,0:T(4,128)S(1)} %get-tuple-element.32), channel_id=1, source_target_pairs={{0,1},{1,0},{2,3},{3,2},{4,5},{5,4},{6,7},{7,6},{8,9},{9,8},{10,11... | collective-permute-start | bytes 110600 | tf_op jit(solution)/shard_map/ppermute | solution.py:362
  43.4 11.1 %all-to-all-start.2 = ((f32[8,1,128]{2,1,0:T(1,128)}), f32[8,1,128]{2,1,0:T(1,128)S(1)}, u32[]{:S(2)}, u32[]{:S(2)}) async-start(f32[8,1,128]{2,1,0:T(1,128)} %bitcast.7), calls=%async_computation.2 | async-start | bytes 8192 | tf_op jit(solution)/shard_map/all_to_all | solution.py:366
  49.9 10.7 %collective-permute-start.7 = (f32[64,128]{1,0:T(8,128)S(1)}, f32[64,128]{1,0:T(8,128)S(1)}, u32[]{:S(2)}, u32[]{:S(2)}) collective-permute-start(f32[64,128]{1,0:T(8,128)S(1)} %get-tuple-element.30), channel_id=1, source_target_pairs={{0,2},{4,6},{2,0},{6,4},{1,3},{5,7},{3,1},{7,5},{8,10},{12,14},{10... | collective-permute-start | bytes 98312 | tf_op jit(solution)/shard_map/ppermute | solution.py:360
  49.9 10.7 %collective-permute-start.8 = (f32[64,128]{1,0:T(8,128)S(1)}, f32[64,128]{1,0:T(8,128)S(1)}, u32[]{:S(2)}, u32[]{:S(2)}) collective-permute-start(f32[64,128]{1,0:T(8,128)S(1)} %get-tuple-element.31), channel_id=1, source_target_pairs={{2,4},{6,0},{4,2},{0,6},{3,5},{7,1},{5,3},{1,7},{10,12},{14,8},{12... | collective-permute-start | bytes 98312 | tf_op jit(solution)/shard_map/ppermute | solution.py:361
  55.1 14.1 %all-to-all-start.3 = ((f32[32,1,128]{2,1,0:T(1,128)}), f32[32,1,128]{2,1,0:T(1,128)S(1)}, u32[]{:S(2)}, u32[]{:S(2)}) async-start(f32[32,1,128]{2,1,0:T(1,128)} %bitcast.10), calls=%async_computation.3 | async-start | bytes 32768 | tf_op jit(solution)/shard_map/all_to_all | solution.py:366

commit v3 on v2

v3 whole, which is shorter than its diff:
```python
import numpy as np
import jax
import jax.numpy as jnp
from jax import lax
from jax.experimental import pallas as pl
from jax.experimental.pallas import tpu as pltpu
from jax.sharding import PartitionSpec as P


ENTRY_LIMIT = 53 * 1024 * 1024
COURANT = 0.4
SPEED_TOTAL = 1.72
SPEED_X, SPEED_Z, SPEED_Y = 0.6, 0.64, 0.48
ROWS = 8


def root_table(degree):
    points = np.cos((np.arange(400) + 0.5) * np.pi / 400)
    values = np.cos(2.0 / 3.0 * np.arccos(0.5 * (points + 1.0)))
    fit = np.polynomial.chebyshev.Chebyshev.fit(points, values, degree, domain=[-1, 1])
    return [float(c) for c in fit.convert(kind=np.polynomial.Polynomial).coef]


ROOT = root_table(11)


def cos_third(ratio):
    half = jnp.sqrt(jnp.maximum(0.5 + 0.5 * ratio, 0.0))
    t = 2.0 * half - 1.0
    total = jnp.full_like(t, ROOT[-1])
    for c in ROOT[-2::-1]:
        total = total * t + c
    return total


def limited(a, b):
    return jnp.maximum(jnp.minimum(a, b), 0.0) + jnp.minimum(jnp.maximum(a, b), 0.0)


def side_terms(c, wm2, wm1, w, wp1, wp2, um1, u, up1):
    d0, d1, d2, d3 = wm1 - wm2, w - wm1, wp1 - w, wp2 - wp1
    below = limited(d0, d1)
    here = (0.5 * c) * limited(d1, d2)
    above = limited(d2, d3)
    base = c * w
    own = (base + here) * jnp.maximum(u, 0.0) - (base - here) * jnp.minimum(u, 0.0)
    low = (wm1 + 0.5 * below) * (c * jnp.minimum(-um1, 0.0))
    high = (wp1 - 0.5 * above) * (c * jnp.minimum(up1, 0.0))
    return own, low, high


def odd_along(axis):
    return lax.rem(lax.axis_index(axis), 2)


def plane_at(x, odd):
    return x + odd * (3 - 2 * x)


class Nodes:
    def __init__(self, a, b, inner):
        self.a, self.b, self.inner = a, b, inner

    def w(self, n, x):
        return (self.a if x >= 2 else self.b).at[n if x in (0, 3) else 6 + n]

    def u(self, n, x):
        if x in (0, 3):
            return (self.a if x == 3 else self.b).at[3 + n]
        return self.inner.at[n if x == 2 else 3 + n]


def rows_of(i):
    return pl.ds(pl.multiple_of(i * ROWS, ROWS), ROWS)


def add_powers(total, parts):
    done = []
    for order in range(6):
        term = parts[0][0]
        for value, _ in parts[1:]:
            term = term + value
        done.append(term if total is None else total[order] + term)
        if order < 5:
            parts = [(value * speed, speed) for value, speed in parts]
    return done


def cross_kernel(a, b, inner, xa, xb, zr, out, pw, pu):
    nodes, sign = Nodes(a, b, inner), 1.0 - 2.0 * odd_along("gx").astype(jnp.float32)

    def plane_w(n, x):
        if x in (-1, 4):
            return (xa if x == 4 else xb).at[n]
        if x in (-2, 5):
            return (xa if x == 5 else xb).at[6 + n]
        return nodes.w(n, x)

    def plane_u(n, x):
        if x in (-1, 4):
            return (xa if x == 4 else xb).at[3 + n]
        return nodes.u(n, x)

    def copy(i, carry):
        zp = pl.ds(pl.multiple_of(i * ROWS + 8, ROWS), ROWS)
        for n in range(3):
            for x in range(4):
                pw[n, x, zp, :] = nodes.w(n, x)[rows_of(i), :]
                pu[n, x, zp, :] = nodes.u(n, x)[rows_of(i), :]
        return carry

    lax.fori_loop(0, 64 // ROWS, copy, 0)
    pw[:, :, 7, :] = zr[0, 0:3]
    pu[:, :, 7, :] = zr[0, 3:6]
    pw[:, :, 6, :] = zr[0, 6:9]
    pw[:, :, 72, :] = zr[1, 0:3]
    pu[:, :, 72, :] = zr[1, 3:6]
    pw[:, :, 73, :] = zr[1, 6:9]

    def rows(i, carry):
        z = rows_of(i)
        for x in range(4):
            total = None
            for n in range(3):
                w, u = nodes.w(n, x)[z, :], nodes.u(n, x)[z, :]
                um1, up1 = plane_u(n, x - 1)[z, :], plane_u(n, x + 1)[z, :]
                own, low, high = side_terms(
                    SPEED_X, plane_w(n, x - 2)[z, :], plane_w(n, x - 1)[z, :], w,
                    plane_w(n, x + 1)[z, :], plane_w(n, x + 2)[z, :], sign * um1, sign * u, sign * up1)
                parts = [(low, um1), (high, up1)]

                def row(ref, s):
                    return ref[n, x, pl.ds(i * ROWS + 8 + s, ROWS), :]

                um1, up1 = row(pu, -1), row(pu, 1)
                own_z, low, high = side_terms(
                    SPEED_Z, row(pw, -2), row(pw, -1), w, row(pw, 1), row(pw, 2), um1, u, up1)
                parts += [(low, um1), (high, up1), (own + own_z, u)]
                total = add_powers(total, parts)
            for k in range(6):
                out[k, x, z, :] = total[k]
        return carry

    lax.fori_loop(0, 64 // ROWS, rows, 0)


def along_kernel(change, a, b, inner, ya, yb, out):
    nodes, flip, lane = Nodes(a, b, inner), odd_along("gy") == 1, lanes()
    first, final = lane == 0, lane == 127

    def rows(i, carry):
        z = rows_of(i)
        va, vb = ya[z, :], yb[z, :]
        below, above = jnp.where(flip, va, vb), jnp.where(flip, vb, va)
        edge = jnp.where(lane % 4 >= 2, above, pltpu.roll(below, 4, 1))
        for x in range(4):
            total = [change[k, x, z, :] for k in range(6)]
            for n in range(3):
                w, u = nodes.w(n, x)[z, :], nodes.u(n, x)[z, :]
                outer = pltpu.roll(edge, 124 - 4 * (3 * x + n), 1)
                wm2 = jnp.where(lane < 2, outer, pltpu.roll(w, 2, 1))
                wp2 = jnp.where(lane >= 126, outer, pltpu.roll(w, 126, 1))
                wm1 = jnp.where(first, pltpu.roll(outer, 127, 1), pltpu.roll(w, 1, 1))
                wp1 = jnp.where(final, pltpu.roll(outer, 1, 1), pltpu.roll(w, 127, 1))
                at = 48 + 2 * (3 * x + n)
                um1 = jnp.where(first, pltpu.roll(below, 128 - at, 1), pltpu.roll(u, 1, 1))
                up1 = jnp.where(final, pltpu.roll(above, 126 - at, 1), pltpu.roll(u, 127, 1))
                own, low, high = side_terms(SPEED_Y, wm2, wm1, w, wp1, wp2, um1, u, up1)
                total = add_powers(total, [(low, um1), (high, up1), (own, u)])
            for k in range(6):
                out[k, x, z, :] = total[k]
        return carry

    lax.fori_loop(0, 64 // ROWS, rows, 0)


def moments_of(nodes):
    total = [None] * 6
    for w, u in nodes:
        power = w
        for order in range(6):
            total[order] = power if total[order] is None else total[order] + power
            if order < 5:
                power = power * u
    return total


def invert(mom):
    inv0 = 1.0 / mom[0]
    a0 = mom[1] * inv0
    s1 = [None] + [mom[l + 1] - a0 * mom[l] for l in range(1, 5)]
    inv1 = 1.0 / s1[1]
    quot = s1[2] * inv1
    a1 = quot - a0
    b1 = s1[1] * inv0
    s2_two = s1[3] - a1 * s1[2] - b1 * mom[2]
    s2_three = s1[4] - a1 * s1[3] - b1 * mom[3]
    a2 = s2_three / s2_two - quot
    b2 = s2_two * inv1
    q = (a0 + a1 + a2) * (1.0 / 3.0)
    d0, d1, d2 = a0 - q, a1 - q, a2 - q
    square = (d0 * d0 + d1 * d1 + d2 * d2 + 2.0 * b1 + 2.0 * b2) * (1.0 / 6.0)
    p = jnp.sqrt(square)
    det = d0 * d1 * d2 - d0 * b2 - d2 * b1
    ratio = det / (2.0 * square * p)
    high = q + 2.0 * p * cos_third(ratio)
    low = q - 2.0 * p * cos_third(-ratio)
    middle = 3.0 * q - high - low
    both = b1 * b2
    scale = mom[0] * both
    nodes = []
    for value in (low, middle, high):
        e0 = value - a0
        e1 = (value - a1) * e0 - b1
        nodes.append((scale / (both + b2 * (e0 * e0) + e1 * e1), value))
    return nodes


def lanes():
    return lax.broadcasted_iota(jnp.int32, (ROWS, 128), 1)


def write_top(top, mx):
    mx[...] = jnp.full(mx.shape, jnp.max(top), jnp.float32)


def step_of(received):
    top = jnp.max(received[...], axis=0, keepdims=True)
    return COURANT / (SPEED_TOTAL * top)


def relay_kernel(got, mx):
    mx[...] = jnp.broadcast_to(jnp.max(got[...], axis=0, keepdims=True), mx.shape)


def entry_kernel(w, u, a, b, inner, zs, mx, sems):
    nodes = Nodes(a, b, inner)
    odd = odd_along("gx")
    loads = [
        pltpu.make_async_copy(array.at[n, plane_at(x, odd)], side(n, x), sems.at[at, n, x])
        for at, (array, side) in enumerate(((u, nodes.u), (w, nodes.w)))
        for n in range(3) for x in range(4)
    ]
    for copy in loads:
        copy.start()
    top = jnp.zeros((ROWS, 128), jnp.float32)
    for at in range(12):
        loads[at].wait()
        for i in range(64 // ROWS):
            top = jnp.maximum(top, jnp.abs(nodes.u(at // 4, at % 4)[i * ROWS:(i + 1) * ROWS, :]))
    write_top(top, mx)
    for copy in loads[12:]:
        copy.wait()
    write_rows(nodes, zs)


def write_rows(nodes, zs):
    for n in range(3):
        for x in range(4):
            w, u = nodes.w(n, x), nodes.u(n, x)
            for k, side, top, bottom in ((n, w, 63, 0), (3 + n, u, 63, 0), (6 + n, w, 62, 1)):
                zs[0, k, x, :] = side[top, :]
                zs[1, k, x, :] = side[bottom, :]


def edge_kernel(a, b, inner, ys):
    nodes, lane = Nodes(a, b, inner), lanes()

    def rows(i, carry):
        z = rows_of(i)
        packed = jnp.zeros((ROWS, 128), jnp.float32)
        for x in range(4):
            for n in range(3):
                at = 3 * x + n
                packed = jnp.where(lane // 4 == at, pltpu.roll(nodes.w(n, x)[z, :], 4 * at + 2, 1), packed)
                packed = jnp.where(lane // 2 == 24 + at, pltpu.roll(nodes.u(n, x)[z, :], 49 + 2 * at, 1), packed)
        ys[z, :] = packed
        return carry

    lax.fori_loop(0, 64 // ROWS, rows, 0)


def middle_kernel(change, a, b, inner, got, base, mid_a, mid_b, mid_inner, zs, mx):
    step = step_of(got)
    old, new = Nodes(a, b, inner), Nodes(mid_a, mid_b, mid_inner)

    def rows(i, top):
        z = rows_of(i)
        for x in range(4):
            mid = []
            for k, moment in enumerate(moments_of([(old.w(n, x)[z, :], old.u(n, x)[z, :]) for n in range(3)])):
                mid.append(moment - step * change[k, x, z, :])
                base[k, x, z, :] = 0.5 * (moment + mid[k])
            for n, (weight, speed) in enumerate(invert(mid)):
                new.w(n, x)[z, :] = weight
                new.u(n, x)[z, :] = speed
                top = jnp.maximum(top, jnp.abs(speed))
        return top

    top = lax.fori_loop(0, 64 // ROWS, rows, jnp.zeros((ROWS, 128), jnp.float32))
    write_top(top, mx)
    write_rows(new, zs)


def exit_kernel(change, base, got, out, held, sems):
    half = 0.5 * step_of(got)
    odd = odd_along("gx")
    stores = []
    for k in range(6):
        for x in range(4):
            held[k, x] = base[k, x] - half * change[k, x]
            stores.append(pltpu.make_async_copy(held.at[k, x], out.at[k, plane_at(x, odd)], sems.at[k, x]))
            stores[-1].start()
    for copy in stores:
        copy.wait()


def f32(*shape):
    return jax.ShapeDtypeStruct(shape, jnp.float32)


PLANES = (f32(9, 64, 128), f32(9, 64, 128), f32(6, 64, 128))
ROWS_Z = f32(2, 9, 4, 128)
MOMENTS = f32(6, 4, 64, 128)
PADDED = [pltpu.VMEM((3, 4, 80, 128), jnp.float32)] * 2
VM = pl.BlockSpec(memory_space=pltpu.VMEM)
ANY = pl.BlockSpec(memory_space=pltpu.HBM)


def call(kernel, outs, args, scratch=(), ins=VM, out=VM, flops=1, limit=8 * 1024 * 1024):
    return pl.pallas_call(
        kernel,
        out_shape=outs,
        in_specs=[ins] * len(args),
        out_specs=out if isinstance(out, tuple) else jax.tree.map(lambda _: out, outs),
        scratch_shapes=list(scratch),
        cost_estimate=pl.CostEstimate(flops=flops, bytes_accessed=1 << 20, transcendentals=0),
        compiler_params=pltpu.CompilerParams(vmem_limit_bytes=limit),
    )(*args)


def pairs(n, first):
    return [(i, (i + 1) % n) for i in range(first, n, 2)] + [((i + 1) % n, i) for i in range(first, n, 2)]


def local(weights, abscissas):
    nx, ny, nz = (lax.axis_size(a) for a in ("gx", "gy", "gz"))
    swap = [(i, (i + 1) % nz) for i in range(nz)]

    def exchange(a, b, inner, zs):
        ys = call(edge_kernel, f32(64, 128), (a, b, inner), flops=1 << 20)
        return (
            lax.ppermute(a, "gx", pairs(nx, 0)),
            lax.ppermute(b, "gx", pairs(nx, 1)),
            lax.ppermute(zs, "gz", swap),
            lax.ppermute(ys, "gy", pairs(ny, 0)),
            lax.ppermute(ys, "gy", pairs(ny, 1)),
        )

    def change_of(planes, xa, xb, zr, ya, yb):
        change = call(cross_kernel, MOMENTS, (*planes, xa, xb, zr), PADDED, flops=4 << 20)
        return call(along_kernel, MOMENTS, (change, *planes, ya, yb), flops=2 << 20)

    def spread(top, axes, n):
        return lax.all_to_all(top.reshape(n, 1, 128), axes, 0, 0).reshape(n, 128)

    def largest(top):
        got = spread(top, ("gy", "gz"), ny * nz)
        top = call(relay_kernel, f32(nx, 128), (got,))
        return spread(top, ("gx",), nx)

    tops = f32(ny * nz, 128)
    *planes, zs, top = call(
        entry_kernel, PLANES + (ROWS_Z, tops), (weights, abscissas),
        [pltpu.SemaphoreType.DMA((2, 3, 4))], ins=ANY, limit=ENTRY_LIMIT)
    halo = exchange(*planes, zs)
    got = largest(top)
    change = change_of(planes, *halo)
    base, *planes, zs, top = call(
        middle_kernel, (MOMENTS,) + PLANES + (ROWS_Z, tops), (change, *planes, got), flops=4 << 20)
    halo = exchange(*planes, zs)
    got = largest(top)
    change = change_of(planes, *halo)
    return call(
        exit_kernel, MOMENTS, (change, base, got),
        [pltpu.VMEM((6, 4, 64, 128), jnp.float32), pltpu.SemaphoreType.DMA((6, 4))], out=ANY)


def solution(mesh):
    spec = P(None, "gx", "gz", "gy")
    return jax.shard_map(local, mesh=mesh, in_specs=(spec, spec), out_specs=spec, check_vma=False)
```

time: 70.6 us -> 68.1 us (0.965)
  waiting for transfers between devices: 15.9 us -> 11.9 us
  Pallas kernels: 15.2 us -> 16.7 us
    all_to_all x4, waiting for transfers between devices: 15.9 us -> 11.8 us  [spread(): return lax.all_to_all(top.reshape(n, 1, 128), axes, 0, 0).reshape(n, 128)]
    pallas_call x9 -> x11, Pallas kernels: 15.2 us -> 16.7 us  [call(): pl.pallas_call(kernel, out_shape=outs, in_specs=[ins] * len(args), out_sp...]
  transfers between devices with their start and end apart: 14 -> 14, of which waited for: 4 -> 4; matrix products, arithmetic and copies ran while one was open for 0% -> 0% of each run, Pallas kernels for 14% -> 17%
where the time goes in v3:
time: 68.1 us; the launch traced here: 67.7 us
  starting transfers between devices  39 us (57%)
  Pallas kernels  16.7 us (25%)
  waiting for transfers between devices  11.9 us (17%)
    all_to_all x4, starting transfers between devices, spread(): return lax.all_to_all(top.reshape(n, 1, 128), axes, 0, 0).reshape(n, 128)  21 us
    pallas_call x11, Pallas kernels, call(): pl.pallas_call(kernel, out_shape=outs, in_specs=[ins] * len(args), out_sp...  16.7 us
    all_to_all x4, waiting for transfers between devices, spread(): return lax.all_to_all(top.reshape(n, 1, 128), axes, 0, 0).reshape(n, 128)  11.8 us
    ppermute x2, starting transfers between devices, exchange(): lax.ppermute(b, 'gx', pairs(nx, 1))  8.13 us
    ppermute x2, starting transfers between devices, exchange(): lax.ppermute(zs, 'gz', swap)  3.65 us
    ppermute x2, starting transfers between devices, exchange(): lax.ppermute(ys, 'gy', pairs(ny, 1))  3.41 us
    ppermute x2, starting transfers between devices, exchange(): lax.ppermute(a, 'gx', pairs(nx, 0))  2.5 us
  transfers between devices with their start and end apart: 14, of which 4 were waited for; matrix products, arithmetic and copies ran while one was open for 0% of the time, Pallas kernels for 17%

profile of v3, /device:TPU:1, one launch (start us, length us, event | category | flops | bytes accessed | tf_op | source)
XLA Modules:
  0.0 67.7 jit_solution(7594206989417956116)
XLA Ops:
  0.0 1.9 %shard_map.28 = (f32[9,64,128]{2,1,0:T(8,128)S(1)}, f32[9,64,128]{2,1,0:T(8,128)S(1)}, f32[6,64,128]{2,1,0:T(8,128)S(1)}, f32[2,9,4,128]{3,2,1,0:T(4,128)S(1)}, f32[8,128]{1,0:T(8,128)}) custom-call(f32[3,4,64,128]{3,2,1,0:T(8,128)} %w.1, f32[3,4,64,128]{3,2,1,0:T(8,128)} %u.1), custom_call_target="tpu_custom_call" | custom-call | flops 1 | bytes 1048576 | tf_op jit(solution)/shard_map/pallas_call | solution.py:331
  1.9 2.2 %collective-permute-start = (f32[9,64,128]{2,1,0:T(8,128)S(1)}, f32[9,64,128]{2,1,0:T(8,128)S(1)}, u32[]{:S(2)}, u32[]{:S(2)}) collective-permute-start(f32[9,64,128]{2,1,0:T(8,128)S(1)} %get-tuple-element.16.a), channel_id=1, source_target_pairs={{0,8},{16,24},{32,40},{48,56},{64,72},{80,88},{96,104},{112,120},{... | collective-permute-start | bytes 884744 | tf_op jit(solution)/shard_map/ppermute | solution.py:353
  4.1 7.2 %collective-permute-start.1 = (f32[9,64,128]{2,1,0:T(8,128)S(1)}, f32[9,64,128]{2,1,0:T(8,128)S(1)}, u32[]{:S(2)}, u32[]{:S(2)}) collective-permute-start(f32[9,64,128]{2,1,0:T(8,128)S(1)} %get-tuple-element.17.b), channel_id=1, source_target_pairs={{8,16},{24,32},{40,48},{56,64},{72,80},{88,96},{104,112},{120,128}... | collective-permute-start | bytes 884744 | tf_op jit(solution)/shard_map/ppermute | solution.py:354
  11.3 2.7 %collective-permute-start.2 = (f32[2,9,4,128]{3,2,1,0:T(4,128)S(1)}, f32[2,9,4,128]{3,2,1,0:T(4,128)S(1)}, u32[]{:S(2)}, u32[]{:S(2)}) collective-permute-start(f32[2,9,4,128]{3,2,1,0:T(4,128)S(1)} %get-tuple-element.19), channel_id=1, source_target_pairs={{0,1},{1,0},{2,3},{3,2},{4,5},{5,4},{6,7},{7,6},{8,9},{9,8},{10,11... | collective-permute-start | bytes 110600 | tf_op jit(solution)/shard_map/ppermute | solution.py:355
  14.0 4.7 %all-to-all-start = ((f32[8,1,128]{2,1,0:T(1,128)}), f32[8,1,128]{2,1,0:T(1,128)S(1)}, u32[]{:S(2)}, u32[]{:S(2)}) async-start(f32[8,1,128]{2,1,0:T(1,128)} %bitcast.1), calls=%async_computation | async-start | bytes 8192 | tf_op jit(solution)/shard_map/all_to_all | solution.py:365
  18.8 0.7 %shard_map.30 = f32[64,128]{1,0:T(8,128)S(1)} custom-call(f32[9,64,128]{2,1,0:T(8,128)S(1)} %get-tuple-element.16.a, f32[9,64,128]{2,1,0:T(8,128)S(1)} %get-tuple-element.17.b, f32[6,64,128]{2,1,0:T(8,128)S(1)} %get-tuple-element.18.inner), custom_call_target="tpu_custom_call" | custom-call | flops 1048576 | bytes 1048576 | tf_op jit(solution)/shard_map/pallas_call | solution.py:331
  19.7 1.7 %collective-permute-start.4 = (f32[64,128]{1,0:T(8,128)S(1)}, f32[64,128]{1,0:T(8,128)S(1)}, u32[]{:S(2)}, u32[]{:S(2)}) collective-permute-start(f32[64,128]{1,0:T(8,128)S(1)} %shard_map.30), channel_id=1, source_target_pairs={{2,4},{6,0},{4,2},{0,6},{3,5},{7,1},{5,3},{1,7},{10,12},{14,8},{12... | collective-permute-start | bytes 98312 | tf_op jit(solution)/shard_map/ppermute | solution.py:357
  21.4 1.9 %all-to-all-done = f32[8,1,128]{2,1,0:T(1,128)S(1)} async-done(((f32[8,1,128]{2,1,0:T(1,128)}), f32[8,1,128]{2,1,0:T(1,128)S(1)}, u32[]{:S(2)}, u32[]{:S(2)}) %all-to-all-start) | async-done | bytes 4128 | tf_op jit(solution)/shard_map/all_to_all | solution.py:365
  23.9 4.2 %all-to-all-start.1 = ((f32[32,1,128]{2,1,0:T(1,128)}), f32[32,1,128]{2,1,0:T(1,128)S(1)}, u32[]{:S(2)}, u32[]{:S(2)}) async-start(f32[32,1,128]{2,1,0:T(1,128)} %bitcast.4), calls=%async_computation.1 | async-start | bytes 32768 | tf_op jit(solution)/shard_map/all_to_all | solution.py:365
  28.2 1.9 %shard_map.29.change = f32[6,4,64,128]{3,2,1,0:T(8,128)S(1)} custom-call(f32[9,64,128]{2,1,0:T(8,128)S(1)} %get-tuple-element.16.a, f32[9,64,128]{2,1,0:T(8,128)S(1)} %get-tuple-element.17.b, f32[6,64,128]{2,1,0:T(8,128)S(1)} %get-tuple-element.18.inner, f32[9,64,128]{2,1,0:T(8,128)S(1)} %collective-permute-done.xa, ...), custom_call_target="tpu_custom_call" | custom-call | flops 4194304 | bytes 1048576 | tf_op jit(solution)/shard_map/pallas_call | solution.py:331
  30.1 2.6 %shard_map.31.change = f32[6,4,64,128]{3,2,1,0:T(8,128)S(1)} custom-call(f32[6,4,64,128]{3,2,1,0:T(8,128)S(1)} %shard_map.29.change, f32[9,64,128]{2,1,0:T(8,128)S(1)} %get-tuple-element.16.a, f32[9,64,128]{2,1,0:T(8,128)S(1)} %get-tuple-element.17.b, f32[6,64,128]{2,1,0:T(8,128)S(1)} %get-tuple-element.18.inner, f32[64,128]{1,0:T(8,128)S(1)} %collective-permute-done.3.ya, ...), custom_call_target="tpu_custom_call" | custom-call | flops 2097152 | bytes 1048576 | tf_op jit(solution)/shard_map/pallas_call | solution.py:331
  32.7 4.0 %all-to-all-done.1 = f32[32,1,128]{2,1,0:T(1,128)S(1)} async-done(((f32[32,1,128]{2,1,0:T(1,128)}), f32[32,1,128]{2,1,0:T(1,128)S(1)}, u32[]{:S(2)}, u32[]{:S(2)}) %all-to-all-start.1) | async-done | bytes 16416 | tf_op jit(solution)/shard_map/all_to_all | solution.py:365
  36.7 2.0 %shard_map.33 = (f32[6,4,64,128]{3,2,1,0:T(8,128)S(1)}, f32[9,64,128]{2,1,0:T(8,128)S(1)}, f32[9,64,128]{2,1,0:T(8,128)S(1)}, f32[6,64,128]{2,1,0:T(8,128)S(1)},...) custom-call(f32[6,4,64,128]{3,2,1,0:T(8,128)S(1)} %shard_map.31.change, f32[9,64,128]{2,1,0:T(8,128)S(1)} %get-tuple-element.16.a, ...), custom_call_target="tpu_custom_call" | custom-call | flops 4194304 | bytes 1048576 | tf_op jit(solution)/shard_map/pallas_call | solution.py:331
  39.0 0.9 %collective-permute-start.6 = (f32[9,64,128]{2,1,0:T(8,128)S(1)}, f32[9,64,128]{2,1,0:T(8,128)S(1)}, u32[]{:S(2)}, u32[]{:S(2)}) collective-permute-start(f32[9,64,128]{2,1,0:T(8,128)S(1)} %get-tuple-element.22.b), channel_id=1, source_target_pairs={{8,16},{24,32},{40,48},{56,64},{72,80},{88,96},{104,112},{120,128}... | collective-permute-start | bytes 884744 | tf_op jit(solution)/shard_map/ppermute | solution.py:354
  39.9 0.9 %collective-permute-start.7 = (f32[2,9,4,128]{3,2,1,0:T(4,128)S(1)}, f32[2,9,4,128]{3,2,1,0:T(4,128)S(1)}, u32[]{:S(2)}, u32[]{:S(2)}) collective-permute-start(f32[2,9,4,128]{3,2,1,0:T(4,128)S(1)} %get-tuple-element.24), channel_id=1, source_target_pairs={{0,1},{1,0},{2,3},{3,2},{4,5},{5,4},{6,7},{7,6},{8,9},{9,8},{10,11... | collective-permute-start | bytes 110600 | tf_op jit(solution)/shard_map/ppermute | solution.py:355
  40.8 6.5 %all-to-all-start.2 = ((f32[8,1,128]{2,1,0:T(1,128)}), f32[8,1,128]{2,1,0:T(1,128)S(1)}, u32[]{:S(2)}, u32[]{:S(2)}) async-start(f32[8,1,128]{2,1,0:T(1,128)} %bitcast.7), calls=%async_computation.2 | async-start | bytes 8192 | tf_op jit(solution)/shard_map/all_to_all | solution.py:365
  47.4 0.7 %shard_map.35 = f32[64,128]{1,0:T(8,128)S(1)} custom-call(f32[9,64,128]{2,1,0:T(8,128)S(1)} %get-tuple-element.21.a, f32[9,64,128]{2,1,0:T(8,128)S(1)} %get-tuple-element.22.b, f32[6,64,128]{2,1,0:T(8,128)S(1)} %get-tuple-element.23.inner), custom_call_target="tpu_custom_call" | custom-call | flops 1048576 | bytes 1048576 | tf_op jit(solution)/shard_map/pallas_call | solution.py:331
  48.2 1.7 %collective-permute-start.9 = (f32[64,128]{1,0:T(8,128)S(1)}, f32[64,128]{1,0:T(8,128)S(1)}, u32[]{:S(2)}, u32[]{:S(2)}) collective-permute-start(f32[64,128]{1,0:T(8,128)S(1)} %shard_map.35), channel_id=1, source_target_pairs={{2,4},{6,0},{4,2},{0,6},{3,5},{7,1},{5,3},{1,7},{10,12},{14,8},{12... | collective-permute-start | bytes 98312 | tf_op jit(solution)/shard_map/ppermute | solution.py:357
  50.0 1.9 %all-to-all-done.2 = f32[8,1,128]{2,1,0:T(1,128)S(1)} async-done(((f32[8,1,128]{2,1,0:T(1,128)}), f32[8,1,128]{2,1,0:T(1,128)S(1)}, u32[]{:S(2)}, u32[]{:S(2)}) %all-to-all-start.2) | async-done | bytes 4128 | tf_op jit(solution)/shard_map/all_to_all | solution.py:365
  52.5 5.6 %all-to-all-start.3 = ((f32[32,1,128]{2,1,0:T(1,128)}), f32[32,1,128]{2,1,0:T(1,128)S(1)}, u32[]{:S(2)}, u32[]{:S(2)}) async-start(f32[32,1,128]{2,1,0:T(1,128)} %bitcast.10), calls=%async_computation.3 | async-start | bytes 32768 | tf_op jit(solution)/shard_map/all_to_all | solution.py:365
  58.1 1.9 %shard_map.34.change = f32[6,4,64,128]{3,2,1,0:T(8,128)S(1)} custom-call(f32[9,64,128]{2,1,0:T(8,128)S(1)} %get-tuple-element.21.a, f32[9,64,128]{2,1,0:T(8,128)S(1)} %get-tuple-element.22.b, f32[6,64,128]{2,1,0:T(8,128)S(1)} %get-tuple-element.23.inner, f32[9,64,128]{2,1,0:T(8,128)S(1)} %collective-permute-done.5.xa, ...), custom_call_target="tpu_custom_call" | custom-call | flops 4194304 | bytes 1048576 | tf_op jit(solution)/shard_map/pallas_call | solution.py:331
  60.0 2.6 %shard_map.36.change = f32[6,4,64,128]{3,2,1,0:T(8,128)S(1)} custom-call(f32[6,4,64,128]{3,2,1,0:T(8,128)S(1)} %shard_map.34.change, f32[9,64,128]{2,1,0:T(8,128)S(1)} %get-tuple-element.21.a, f32[9,64,128]{2,1,0:T(8,128)S(1)} %get-tuple-element.22.b, f32[6,64,128]{2,1,0:T(8,128)S(1)} %get-tuple-element.23.inner, f32[64,128]{1,0:T(8,128)S(1)} %collective-permute-done.8.ya, ...), custom_call_target="tpu_custom_call" | custom-call | flops 2097152 | bytes 1048576 | tf_op jit(solution)/shard_map/pallas_call | solution.py:331
  62.6 4.0 %all-to-all-done.3 = f32[32,1,128]{2,1,0:T(1,128)S(1)} async-done(((f32[32,1,128]{2,1,0:T(1,128)}), f32[32,1,128]{2,1,0:T(1,128)S(1)}, u32[]{:S(2)}, u32[]{:S(2)}) %all-to-all-start.3) | async-done | bytes 16416 | tf_op jit(solution)/shard_map/all_to_all | solution.py:365
  66.6 1.1 %shard_map.38 = f32[6,4,64,128]{3,2,1,0:T(8,128)} custom-call(f32[6,4,64,128]{3,2,1,0:T(8,128)S(1)} %shard_map.36.change, f32[6,4,64,128]{3,2,1,0:T(8,128)S(1)} %get-tuple-element.25.base, f32[32,128]{1,0:T(8,128)S(1)} %bitcast.17), custom_call_target="tpu_custom_call" | custom-call | flops 1 | bytes 1048576 | tf_op jit(solution)/shard_map/pallas_call | solution.py:331
  (15 shorter events, 1.8 us)
Async XLA Ops:
  1.9 26.3 %collective-permute-start = (f32[9,64,128]{2,1,0:T(8,128)S(1)}, f32[9,64,128]{2,1,0:T(8,128)S(1)}, u32[]{:S(2)}, u32[]{:S(2)}) collective-permute-start(f32[9,64,128]{2,1,0:T(8,128)S(1)} %get-tuple-element.16.a), channel_id=1, source_target_pairs={{0,8},{16,24},{32,40},{48,56},{64,72},{80,88},{96,104},{112,120},{... | collective-permute-start | bytes 884744 | tf_op jit(solution)/shard_map/ppermute | solution.py:353
  4.1 24.1 %collective-permute-start.1 = (f32[9,64,128]{2,1,0:T(8,128)S(1)}, f32[9,64,128]{2,1,0:T(8,128)S(1)}, u32[]{:S(2)}, u32[]{:S(2)}) collective-permute-start(f32[9,64,128]{2,1,0:T(8,128)S(1)} %get-tuple-element.17.b), channel_id=1, source_target_pairs={{8,16},{24,32},{40,48},{56,64},{72,80},{88,96},{104,112},{120,128}... | collective-permute-start | bytes 884744 | tf_op jit(solution)/shard_map/ppermute | solution.py:354
  11.3 16.9 %collective-permute-start.2 = (f32[2,9,4,128]{3,2,1,0:T(4,128)S(1)}, f32[2,9,4,128]{3,2,1,0:T(4,128)S(1)}, u32[]{:S(2)}, u32[]{:S(2)}) collective-permute-start(f32[2,9,4,128]{3,2,1,0:T(4,128)S(1)} %get-tuple-element.19), channel_id=1, source_target_pairs={{0,1},{1,0},{2,3},{3,2},{4,5},{5,4},{6,7},{7,6},{8,9},{9,8},{10,11... | collective-permute-start | bytes 110600 | tf_op jit(solution)/shard_map/ppermute | solution.py:355
  14.0 9.3 %all-to-all-start = ((f32[8,1,128]{2,1,0:T(1,128)}), f32[8,1,128]{2,1,0:T(1,128)S(1)}, u32[]{:S(2)}, u32[]{:S(2)}) async-start(f32[8,1,128]{2,1,0:T(1,128)} %bitcast.1), calls=%async_computation | async-start | bytes 8192 | tf_op jit(solution)/shard_map/all_to_all | solution.py:365
  19.5 10.5 %collective-permute-start.3 = (f32[64,128]{1,0:T(8,128)S(1)}, f32[64,128]{1,0:T(8,128)S(1)}, u32[]{:S(2)}, u32[]{:S(2)}) collective-permute-start(f32[64,128]{1,0:T(8,128)S(1)} %shard_map.30), channel_id=1, source_target_pairs={{0,2},{4,6},{2,0},{6,4},{1,3},{5,7},{3,1},{7,5},{8,10},{12,14},{10... | collective-permute-start | bytes 98312 | tf_op jit(solution)/shard_map/ppermute | solution.py:356
  19.7 10.3 %collective-permute-start.4 = (f32[64,128]{1,0:T(8,128)S(1)}, f32[64,128]{1,0:T(8,128)S(1)}, u32[]{:S(2)}, u32[]{:S(2)}) collective-permute-start(f32[64,128]{1,0:T(8,128)S(1)} %shard_map.30), channel_id=1, source_target_pairs={{2,4},{6,0},{4,2},{0,6},{3,5},{7,1},{5,3},{1,7},{10,12},{14,8},{12... | collective-permute-start | bytes 98312 | tf_op jit(solution)/shard_map/ppermute | solution.py:357
  23.9 12.8 %all-to-all-start.1 = ((f32[32,1,128]{2,1,0:T(1,128)}), f32[32,1,128]{2,1,0:T(1,128)S(1)}, u32[]{:S(2)}, u32[]{:S(2)}) async-start(f32[32,1,128]{2,1,0:T(1,128)} %bitcast.4), calls=%async_computation.1 | async-start | bytes 32768 | tf_op jit(solution)/shard_map/all_to_all | solution.py:365
  38.7 19.4 %collective-permute-start.5 = (f32[9,64,128]{2,1,0:T(8,128)S(1)}, f32[9,64,128]{2,1,0:T(8,128)S(1)}, u32[]{:S(2)}, u32[]{:S(2)}) collective-permute-start(f32[9,64,128]{2,1,0:T(8,128)S(1)} %get-tuple-element.21.a), channel_id=1, source_target_pairs={{0,8},{16,24},{32,40},{48,56},{64,72},{80,88},{96,104},{112,120},{... | collective-permute-start | bytes 884744 | tf_op jit(solution)/shard_map/ppermute | solution.py:353
  39.0 19.1 %collective-permute-start.6 = (f32[9,64,128]{2,1,0:T(8,128)S(1)}, f32[9,64,128]{2,1,0:T(8,128)S(1)}, u32[]{:S(2)}, u32[]{:S(2)}) collective-permute-start(f32[9,64,128]{2,1,0:T(8,128)S(1)} %get-tuple-element.22.b), channel_id=1, source_target_pairs={{8,16},{24,32},{40,48},{56,64},{72,80},{88,96},{104,112},{120,128}... | collective-permute-start | bytes 884744 | tf_op jit(solution)/shard_map/ppermute | solution.py:354
  39.9 18.1 %collective-permute-start.7 = (f32[2,9,4,128]{3,2,1,0:T(4,128)S(1)}, f32[2,9,4,128]{3,2,1,0:T(4,128)S(1)}, u32[]{:S(2)}, u32[]{:S(2)}) collective-permute-start(f32[2,9,4,128]{3,2,1,0:T(4,128)S(1)} %get-tuple-element.24), channel_id=1, source_target_pairs={{0,1},{1,0},{2,3},{3,2},{4,5},{5,4},{6,7},{7,6},{8,9},{9,8},{10,11... | collective-permute-start | bytes 110600 | tf_op jit(solution)/shard_map/ppermute | solution.py:355
  40.8 11.1 %all-to-all-start.2 = ((f32[8,1,128]{2,1,0:T(1,128)}), f32[8,1,128]{2,1,0:T(1,128)S(1)}, u32[]{:S(2)}, u32[]{:S(2)}) async-start(f32[8,1,128]{2,1,0:T(1,128)} %bitcast.7), calls=%async_computation.2 | async-start | bytes 8192 | tf_op jit(solution)/shard_map/all_to_all | solution.py:365
  48.1 11.9 %collective-permute-start.8 = (f32[64,128]{1,0:T(8,128)S(1)}, f32[64,128]{1,0:T(8,128)S(1)}, u32[]{:S(2)}, u32[]{:S(2)}) collective-permute-start(f32[64,128]{1,0:T(8,128)S(1)} %shard_map.35), channel_id=1, source_target_pairs={{0,2},{4,6},{2,0},{6,4},{1,3},{5,7},{3,1},{7,5},{8,10},{12,14},{10... | collective-permute-start | bytes 98312 | tf_op jit(solution)/shard_map/ppermute | solution.py:356
  48.2 11.8 %collective-permute-start.9 = (f32[64,128]{1,0:T(8,128)S(1)}, f32[64,128]{1,0:T(8,128)S(1)}, u32[]{:S(2)}, u32[]{:S(2)}) collective-permute-start(f32[64,128]{1,0:T(8,128)S(1)} %shard_map.35), channel_id=1, source_target_pairs={{2,4},{6,0},{4,2},{0,6},{3,5},{7,1},{5,3},{1,7},{10,12},{14,8},{12... | collective-permute-start | bytes 98312 | tf_op jit(solution)/shard_map/ppermute | solution.py:357
  52.5 14.1 %all-to-all-start.3 = ((f32[32,1,128]{2,1,0:T(1,128)}), f32[32,1,128]{2,1,0:T(1,128)S(1)}, u32[]{:S(2)}, u32[]{:S(2)}) async-start(f32[32,1,128]{2,1,0:T(1,128)} %bitcast.10), calls=%async_computation.3 | async-start | bytes 32768 | tf_op jit(solution)/shard_map/all_to_all | solution.py:365

commit v4 on v3

--- a/solution.py
+++ b/solution.py
@@ -12,6 +12,8 @@
 SPEED_TOTAL = 1.72
 SPEED_X, SPEED_Z, SPEED_Y = 0.6, 0.64, 0.48
 ROWS = 8
+LONG = 32
+EDGE = 64
 
 
 def root_table(degree):
@@ -70,8 +72,8 @@
         return self.inner.at[n if x == 2 else 3 + n]
 
 
-def rows_of(i):
-    return pl.ds(pl.multiple_of(i * ROWS, ROWS), ROWS)
+def rows_of(i, rows=ROWS):
+    return pl.ds(pl.multiple_of(i * rows, rows), rows)
 
 
 def add_powers(total, parts):
@@ -86,6 +88,22 @@
     return done
 
 
+def row_at(side, k, x):
+    return 36 * side + 4 * k + x
+
+
+def write_rows(nodes, top, zs, mx):
+    most = jnp.full(mx.shape, jnp.max(top), jnp.float32)
+    mx[...] = most
+    zs[72:80, :] = most
+    for n in range(3):
+        for x in range(4):
+            w, u = nodes.w(n, x), nodes.u(n, x)
+            for k, side, top, bottom in ((n, w, 63, 0), (3 + n, u, 63, 0), (6 + n, w, 62, 1)):
+                zs[row_at(0, k, x), :] = side[top, :]
+                zs[row_at(1, k, x), :] = side[bottom, :]
+
+
 def cross_kernel(a, b, inner, xa, xb, zr, out, pw, pu):
     nodes, sign = Nodes(a, b, inner), 1.0 - 2.0 * odd_along("gx").astype(jnp.float32)
 
@@ -110,12 +128,14 @@
         return carry
 
     lax.fori_loop(0, 64 // ROWS, copy, 0)
-    pw[:, :, 7, :] = zr[0, 0:3]
-    pu[:, :, 7, :] = zr[0, 3:6]
-    pw[:, :, 6, :] = zr[0, 6:9]
-    pw[:, :, 72, :] = zr[1, 0:3]
-    pu[:, :, 72, :] = zr[1, 3:6]
-    pw[:, :, 73, :] = zr[1, 6:9]
+    for n in range(3):
+        for x in range(4):
+            pw[n, x, 7, :] = zr[row_at(0, n, x), :]
+            pu[n, x, 7, :] = zr[row_at(0, 3 + n, x), :]
+            pw[n, x, 6, :] = zr[row_at(0, 6 + n, x), :]
+            pw[n, x, 72, :] = zr[row_at(1, n, x), :]
+            pu[n, x, 72, :] = zr[row_at(1, 3 + n, x), :]
+            pw[n, x, 73, :] = zr[row_at(1, 6 + n, x), :]
 
     def rows(i, carry):
         z = rows_of(i)
@@ -145,11 +165,11 @@
 
 
 def along_kernel(change, a, b, inner, ya, yb, out):
-    nodes, flip, lane = Nodes(a, b, inner), odd_along("gy") == 1, lanes()
+    nodes, flip, lane = Nodes(a, b, inner), odd_along("gy") == 1, lanes(LONG)
     first, final = lane == 0, lane == 127
 
     def rows(i, carry):
-        z = rows_of(i)
+        z = rows_of(i, LONG)
         va, vb = ya[z, :], yb[z, :]
         below, above = jnp.where(flip, va, vb), jnp.where(flip, vb, va)
         edge = jnp.where(lane % 4 >= 2, above, pltpu.roll(below, 4, 1))
@@ -171,7 +191,7 @@
                 out[k, x, z, :] = total[k]
         return carry
 
-    lax.fori_loop(0, 64 // ROWS, rows, 0)
+    lax.fori_loop(0, 64 // LONG, rows, 0)
 
 
 def moments_of(nodes):
@@ -216,12 +236,8 @@
     return nodes
 
 
-def lanes():
-    return lax.broadcasted_iota(jnp.int32, (ROWS, 128), 1)
-
-
-def write_top(top, mx):
-    mx[...] = jnp.full(mx.shape, jnp.max(top), jnp.float32)
+def lanes(rows=ROWS):
+    return lax.broadcasted_iota(jnp.int32, (rows, 128), 1)
 
 
 def step_of(received):
@@ -229,8 +245,10 @@
     return COURANT / (SPEED_TOTAL * top)
 
 
-def relay_kernel(got, mx):
-    mx[...] = jnp.broadcast_to(jnp.max(got[...], axis=0, keepdims=True), mx.shape)
+def relay_kernel(own, got, mx):
+    most = jnp.maximum(own[...], got[72:80, :])
+    for i in range(mx.shape[0] // ROWS):
+        mx[i * ROWS:(i + 1) * ROWS, :] = most
 
 
 def entry_kernel(w, u, a, b, inner, zs, mx, sems):
@@ -248,27 +266,17 @@
         loads[at].wait()
         for i in range(64 // ROWS):
             top = jnp.maximum(top, jnp.abs(nodes.u(at // 4, at % 4)[i * ROWS:(i + 1) * ROWS, :]))
-    write_top(top, mx)
     for copy in loads[12:]:
         copy.wait()
-    write_rows(nodes, zs)
-
-
-def write_rows(nodes, zs):
-    for n in range(3):
-        for x in range(4):
-            w, u = nodes.w(n, x), nodes.u(n, x)
-            for k, side, top, bottom in ((n, w, 63, 0), (3 + n, u, 63, 0), (6 + n, w, 62, 1)):
-                zs[0, k, x, :] = side[top, :]
-                zs[1, k, x, :] = side[bottom, :]
+    write_rows(nodes, top, zs, mx)
 
 
 def edge_kernel(a, b, inner, ys):
-    nodes, lane = Nodes(a, b, inner), lanes()
+    nodes, lane = Nodes(a, b, inner), lanes(EDGE)
 
     def rows(i, carry):
-        z = rows_of(i)
-        packed = jnp.zeros((ROWS, 128), jnp.float32)
+        z = rows_of(i, EDGE)
+        packed = jnp.zeros((EDGE, 128), jnp.float32)
         for x in range(4):
             for n in range(3):
                 at = 3 * x + n
@@ -277,7 +285,7 @@
         ys[z, :] = packed
         return carry
 
-    lax.fori_loop(0, 64 // ROWS, rows, 0)
+    lax.fori_loop(0, 64 // EDGE, rows, 0)
 
 
 def middle_kernel(change, a, b, inner, got, base, mid_a, mid_b, mid_inner, zs, mx):
@@ -298,8 +306,7 @@
         return top
 
     top = lax.fori_loop(0, 64 // ROWS, rows, jnp.zeros((ROWS, 128), jnp.float32))
-    write_top(top, mx)
-    write_rows(new, zs)
+    write_rows(new, top, zs, mx)
 
 
 def exit_kernel(change, base, got, out, held, sems):
@@ -320,7 +327,7 @@
 
 
 PLANES = (f32(9, 64, 128), f32(9, 64, 128), f32(6, 64, 128))
-ROWS_Z = f32(2, 9, 4, 128)
+ROWS_Z, TOP = f32(80, 128), f32(ROWS, 128)
 MOMENTS = f32(6, 4, 64, 128)
 PADDED = [pltpu.VMEM((3, 4, 80, 128), jnp.float32)] * 2
 VM = pl.BlockSpec(memory_space=pltpu.VMEM)
@@ -347,39 +354,32 @@
     nx, ny, nz = (lax.axis_size(a) for a in ("gx", "gy", "gz"))
     swap = [(i, (i + 1) % nz) for i in range(nz)]
 
-    def exchange(a, b, inner, zs):
+    def exchange(a, b, inner, zs, top):
         ys = call(edge_kernel, f32(64, 128), (a, b, inner), flops=1 << 20)
-        return (
+        halo = (
             lax.ppermute(a, "gx", pairs(nx, 0)),
             lax.ppermute(b, "gx", pairs(nx, 1)),
             lax.ppermute(zs, "gz", swap),
             lax.ppermute(ys, "gy", pairs(ny, 0)),
             lax.ppermute(ys, "gy", pairs(ny, 1)),
         )
+        n = nx * ny
+        top = call(relay_kernel, f32(n, 128), (top, halo[2]))
+        got = lax.all_to_all(top.reshape(n, 1, 128), ("gx", "gy"), 0, 0)
+        return halo, got.reshape(n, 128)
 
     def change_of(planes, xa, xb, zr, ya, yb):
         change = call(cross_kernel, MOMENTS, (*planes, xa, xb, zr), PADDED, flops=4 << 20)
         return call(along_kernel, MOMENTS, (change, *planes, ya, yb), flops=2 << 20)
 
-    def spread(top, axes, n):
-        return lax.all_to_all(top.reshape(n, 1, 128), axes, 0, 0).reshape(n, 128)
-
-    def largest(top):
-        got = spread(top, ("gy", "gz"), ny * nz)
-        top = call(relay_kernel, f32(nx, 128), (got,))
-        return spread(top, ("gx",), nx)
-
-    tops = f32(ny * nz, 128)
     *planes, zs, top = call(
-        entry_kernel, PLANES + (ROWS_Z, tops), (weights, abscissas),
+        entry_kernel, PLANES + (ROWS_Z, TOP), (weights, abscissas),
         [pltpu.SemaphoreType.DMA((2, 3, 4))], ins=ANY, limit=ENTRY_LIMIT)
-    halo = exchange(*planes, zs)
-    got = largest(top)
+    halo, got = exchange(*planes, zs, top)
     change = change_of(planes, *halo)
     base, *planes, zs, top = call(
-        middle_kernel, (MOMENTS,) + PLANES + (ROWS_Z, tops), (change, *planes, got), flops=4 << 20)
-    halo = exchange(*planes, zs)
-    got = largest(top)
+        middle_kernel, (MOMENTS,) + PLANES + (ROWS_Z, TOP), (change, *planes, got), flops=4 << 20)
+    halo, got = exchange(*planes, zs, top)
     change = change_of(planes, *halo)
     return call(
         exit_kernel, MOMENTS, (change, base, got),

time: 68.1 us -> 63.9 us (0.938)
  Pallas kernels: 16.7 us -> 13.9 us
  starting transfers between devices: 39 us -> 37.9 us
    all_to_all x4 -> x2, waiting for transfers between devices: 11.8 us -> 5.96 us  [exchange(): got = lax.all_to_all(top.reshape(n, 1, 128), ('gx', 'gy'), 0, 0)]
    all_to_all x4 -> x2, starting transfers between devices: 21 us -> 17.1 us  [exchange(): got = lax.all_to_all(top.reshape(n, 1, 128), ('gx', 'gy'), 0, 0)]
    ppermute x2, waiting for transfers between devices: 0.01 us -> 3.81 us  [exchange(): lax.ppermute(zs, 'gz', swap)]
    pallas_call x11, Pallas kernels: 16.7 us -> 13.9 us  [call(): pl.pallas_call(kernel, out_shape=outs, in_specs=[ins] * len(args), out_sp...]
    ppermute x2, waiting for transfers between devices: 0.01 us -> 1.92 us  [exchange(): lax.ppermute(ys, 'gy', pairs(ny, 1))]
    ppermute x2, starting transfers between devices: 3.41 us -> 1.71 us  [exchange(): lax.ppermute(ys, 'gy', pairs(ny, 1))]
    ppermute x2, starting transfers between devices: 0.28 us -> 1.96 us  [exchange(): lax.ppermute(ys, 'gy', pairs(ny, 0))]
    ppermute x2, starting transfers between devices: 3.65 us -> 5.19 us  [exchange(): lax.ppermute(zs, 'gz', swap)]
  transfers between devices with their start and end apart: 14 -> 12, of which waited for: 4 -> 6; matrix products, arithmetic and copies ran while one was open for 0% -> 0% of each run, Pallas kernels for 17% -> 16%
where the time goes in v4:
time: 63.9 us; the launch traced here: 63.7 us
  starting transfers between devices  37.9 us (59%)
  Pallas kernels  13.9 us (22%)
  waiting for transfers between devices  11.7 us (18%)
    all_to_all x2, starting transfers between devices, exchange(): got = lax.all_to_all(top.reshape(n, 1, 128), ('gx', 'gy'), 0, 0)  17.1 us
    pallas_call x11, Pallas kernels, call(): pl.pallas_call(kernel, out_shape=outs, in_specs=[ins] * len(args), out_sp...  13.9 us
    ppermute x2, starting transfers between devices, exchange(): lax.ppermute(b, 'gx', pairs(nx, 1))  9.53 us
    all_to_all x2, waiting for transfers between devices, exchange(): got = lax.all_to_all(top.reshape(n, 1, 128), ('gx', 'gy'), 0, 0)  5.96 us
    ppermute x2, starting transfers between devices, exchange(): lax.ppermute(zs, 'gz', swap)  5.19 us
    ppermute x2, waiting for transfers between devices, exchange(): lax.ppermute(zs, 'gz', swap)  3.81 us
    ppermute x2, starting transfers between devices, exchange(): lax.ppermute(a, 'gx', pairs(nx, 0))  2.46 us
    ppermute x2, starting transfers between devices, exchange(): lax.ppermute(ys, 'gy', pairs(ny, 0))  1.96 us
  transfers between devices with their start and end apart: 12, of which 6 were waited for; matrix products, arithmetic and copies ran while one was open for 0% of the time, Pallas kernels for 16%

profile of v4, /device:TPU:1, one launch (start us, length us, event | category | flops | bytes accessed | tf_op | source)
XLA Modules:
  0.0 63.7 jit_solution(18124499022415586373)
XLA Ops:
  0.0 1.4 %shard_map.28 = (f32[9,64,128]{2,1,0:T(8,128)S(1)}, f32[9,64,128]{2,1,0:T(8,128)S(1)}, f32[6,64,128]{2,1,0:T(8,128)S(1)}, f32[80,128]{1,0:T(8,128)S(1)}, f32[8,128]{1,0:T(8,128)S(1)}) custom-call(f32[3,4,64,128]{3,2,1,0:T(8,128)} %w.1, f32[3,4,64,128]{3,2,1,0:T(8,128)} %u.1), custom_call_target="tpu_custom_call" | custom-call | flops 1 | bytes 1048576 | tf_op jit(solution)/shard_map/pallas_call | solution.py:338
  1.4 2.2 %collective-permute-start = (f32[9,64,128]{2,1,0:T(8,128)S(1)}, f32[9,64,128]{2,1,0:T(8,128)S(1)}, u32[]{:S(2)}, u32[]{:S(2)}) collective-permute-start(f32[9,64,128]{2,1,0:T(8,128)S(1)} %get-tuple-element.16.a), channel_id=1, source_target_pairs={{0,8},{16,24},{32,40},{48,56},{64,72},{80,88},{96,104},{112,120},{... | collective-permute-start | bytes 884744 | tf_op jit(solution)/shard_map/ppermute | solution.py:360
  3.6 7.2 %collective-permute-start.1 = (f32[9,64,128]{2,1,0:T(8,128)S(1)}, f32[9,64,128]{2,1,0:T(8,128)S(1)}, u32[]{:S(2)}, u32[]{:S(2)}) collective-permute-start(f32[9,64,128]{2,1,0:T(8,128)S(1)} %get-tuple-element.17.b), channel_id=1, source_target_pairs={{8,16},{24,32},{40,48},{56,64},{72,80},{88,96},{104,112},{120,128}... | collective-permute-start | bytes 884744 | tf_op jit(solution)/shard_map/ppermute | solution.py:361
  10.8 2.7 %collective-permute-start.2 = (f32[80,128]{1,0:T(8,128)S(1)}, f32[80,128]{1,0:T(8,128)S(1)}, u32[]{:S(2)}, u32[]{:S(2)}) collective-permute-start(f32[80,128]{1,0:T(8,128)S(1)} %get-tuple-element.19), channel_id=1, source_target_pairs={{0,1},{1,0},{2,3},{3,2},{4,5},{5,4},{6,7},{7,6},{8,9},{9,8},{10,11... | collective-permute-start | bytes 122888 | tf_op jit(solution)/shard_map/ppermute | solution.py:362
  13.5 1.9 %collective-permute-done.2.zr.got = f32[80,128]{1,0:T(8,128)S(1)} collective-permute-done((f32[80,128]{1,0:T(8,128)S(1)}, f32[80,128]{1,0:T(8,128)S(1)}, u32[]{:S(2)}, u32[]{:S(2)}) %collective-permute-start.2) | collective-permute-done | bytes 40992 | tf_op jit(solution)/shard_map/ppermute | solution.py:362
  16.1 8.5 %all-to-all-start = ((f32[128,1,128]{2,1,0:T(1,128)}), f32[128,1,128]{2,1,0:T(1,128)S(1)}, u32[]{:S(2)}, u32[]{:S(2)}) async-start(f32[128,1,128]{2,1,0:T(1,128)} %bitcast.1), calls=%async_computation | async-start | bytes 131072 | tf_op jit(solution)/shard_map/all_to_all | solution.py:368
  24.8 1.0 %collective-permute-start.3 = (f32[64,128]{1,0:T(8,128)S(1)}, f32[64,128]{1,0:T(8,128)S(1)}, u32[]{:S(2)}, u32[]{:S(2)}) collective-permute-start(f32[64,128]{1,0:T(8,128)S(1)} %shard_map.30), channel_id=1, source_target_pairs={{0,2},{4,6},{2,0},{6,4},{1,3},{5,7},{3,1},{7,5},{8,10},{12,14},{10... | collective-permute-start | bytes 98312 | tf_op jit(solution)/shard_map/ppermute | solution.py:363
  25.8 0.9 %collective-permute-start.4 = (f32[64,128]{1,0:T(8,128)S(1)}, f32[64,128]{1,0:T(8,128)S(1)}, u32[]{:S(2)}, u32[]{:S(2)}) collective-permute-start(f32[64,128]{1,0:T(8,128)S(1)} %shard_map.30), channel_id=1, source_target_pairs={{2,4},{6,0},{4,2},{0,6},{3,5},{7,1},{5,3},{1,7},{10,12},{14,8},{12... | collective-permute-start | bytes 98312 | tf_op jit(solution)/shard_map/ppermute | solution.py:364
  26.7 1.8 %shard_map.29.change = f32[6,4,64,128]{3,2,1,0:T(8,128)S(1)} custom-call(f32[9,64,128]{2,1,0:T(8,128)S(1)} %get-tuple-element.16.a, f32[9,64,128]{2,1,0:T(8,128)S(1)} %get-tuple-element.17.b, f32[6,64,128]{2,1,0:T(8,128)S(1)} %get-tuple-element.18.inner, f32[9,64,128]{2,1,0:T(8,128)S(1)} %collective-permute-done.xa, ...), custom_call_target="tpu_custom_call" | custom-call | flops 4194304 | bytes 1048576 | tf_op jit(solution)/shard_map/pallas_call | solution.py:338
  28.5 1.0 %collective-permute-done.4.yb = f32[64,128]{1,0:T(8,128)S(1)} collective-permute-done((f32[64,128]{1,0:T(8,128)S(1)}, f32[64,128]{1,0:T(8,128)S(1)}, u32[]{:S(2)}, u32[]{:S(2)}) %collective-permute-start.4) | collective-permute-done | bytes 32800 | tf_op jit(solution)/shard_map/ppermute | solution.py:364
  29.5 2.3 %shard_map.31.change = f32[6,4,64,128]{3,2,1,0:T(8,128)S(1)} custom-call(f32[6,4,64,128]{3,2,1,0:T(8,128)S(1)} %shard_map.29.change, f32[9,64,128]{2,1,0:T(8,128)S(1)} %get-tuple-element.16.a, f32[9,64,128]{2,1,0:T(8,128)S(1)} %get-tuple-element.17.b, f32[6,64,128]{2,1,0:T(8,128)S(1)} %get-tuple-element.18.inner, f32[64,128]{1,0:T(8,128)S(1)} %collective-permute-done.3.ya, ...), custom_call_target="tpu_custom_call" | custom-call | flops 2097152 | bytes 1048576 | tf_op jit(solution)/shard_map/pallas_call | solution.py:338
  31.8 3.0 %all-to-all-done = f32[128,1,128]{2,1,0:T(1,128)S(1)} async-done(((f32[128,1,128]{2,1,0:T(1,128)}), f32[128,1,128]{2,1,0:T(1,128)S(1)}, u32[]{:S(2)}, u32[]{:S(2)}) %all-to-all-start) | async-done | bytes 65568 | tf_op jit(solution)/shard_map/all_to_all | solution.py:368
  34.8 1.4 %shard_map.33 = (f32[6,4,64,128]{3,2,1,0:T(8,128)S(1)}, f32[9,64,128]{2,1,0:T(8,128)S(1)}, f32[9,64,128]{2,1,0:T(8,128)S(1)}, f32[6,64,128]{2,1,0:T(8,128)S(1)},...) custom-call(f32[6,4,64,128]{3,2,1,0:T(8,128)S(1)} %shard_map.31.change, f32[9,64,128]{2,1,0:T(8,128)S(1)} %get-tuple-element.16.a, ...), custom_call_target="tpu_custom_call" | custom-call | flops 4194304 | bytes 1048576 | tf_op jit(solution)/shard_map/pallas_call | solution.py:338
  36.5 2.3 %collective-permute-start.6 = (f32[9,64,128]{2,1,0:T(8,128)S(1)}, f32[9,64,128]{2,1,0:T(8,128)S(1)}, u32[]{:S(2)}, u32[]{:S(2)}) collective-permute-start(f32[9,64,128]{2,1,0:T(8,128)S(1)} %get-tuple-element.22.b), channel_id=1, source_target_pairs={{8,16},{24,32},{40,48},{56,64},{72,80},{88,96},{104,112},{120,128}... | collective-permute-start | bytes 884744 | tf_op jit(solution)/shard_map/ppermute | solution.py:361
  38.8 2.5 %collective-permute-start.7 = (f32[80,128]{1,0:T(8,128)S(1)}, f32[80,128]{1,0:T(8,128)S(1)}, u32[]{:S(2)}, u32[]{:S(2)}) collective-permute-start(f32[80,128]{1,0:T(8,128)S(1)} %get-tuple-element.24), channel_id=1, source_target_pairs={{0,1},{1,0},{2,3},{3,2},{4,5},{5,4},{6,7},{7,6},{8,9},{9,8},{10,11... | collective-permute-start | bytes 122888 | tf_op jit(solution)/shard_map/ppermute | solution.py:362
  41.2 1.9 %collective-permute-done.7.zr.got = f32[80,128]{1,0:T(8,128)S(1)} collective-permute-done((f32[80,128]{1,0:T(8,128)S(1)}, f32[80,128]{1,0:T(8,128)S(1)}, u32[]{:S(2)}, u32[]{:S(2)}) %collective-permute-start.7) | collective-permute-done | bytes 40992 | tf_op jit(solution)/shard_map/ppermute | solution.py:362
  43.8 8.6 %all-to-all-start.1 = ((f32[128,1,128]{2,1,0:T(1,128)}), f32[128,1,128]{2,1,0:T(1,128)S(1)}, u32[]{:S(2)}, u32[]{:S(2)}) async-start(f32[128,1,128]{2,1,0:T(1,128)} %bitcast.4), calls=%async_computation.1 | async-start | bytes 131072 | tf_op jit(solution)/shard_map/all_to_all | solution.py:368
  52.7 1.0 %collective-permute-start.8 = (f32[64,128]{1,0:T(8,128)S(1)}, f32[64,128]{1,0:T(8,128)S(1)}, u32[]{:S(2)}, u32[]{:S(2)}) collective-permute-start(f32[64,128]{1,0:T(8,128)S(1)} %shard_map.35), channel_id=1, source_target_pairs={{0,2},{4,6},{2,0},{6,4},{1,3},{5,7},{3,1},{7,5},{8,10},{12,14},{10... | collective-permute-start | bytes 98312 | tf_op jit(solution)/shard_map/ppermute | solution.py:363
  53.7 0.9 %collective-permute-start.9 = (f32[64,128]{1,0:T(8,128)S(1)}, f32[64,128]{1,0:T(8,128)S(1)}, u32[]{:S(2)}, u32[]{:S(2)}) collective-permute-start(f32[64,128]{1,0:T(8,128)S(1)} %shard_map.35), channel_id=1, source_target_pairs={{2,4},{6,0},{4,2},{0,6},{3,5},{7,1},{5,3},{1,7},{10,12},{14,8},{12... | collective-permute-start | bytes 98312 | tf_op jit(solution)/shard_map/ppermute | solution.py:364
  54.5 1.8 %shard_map.34.change = f32[6,4,64,128]{3,2,1,0:T(8,128)S(1)} custom-call(f32[9,64,128]{2,1,0:T(8,128)S(1)} %get-tuple-element.21.a, f32[9,64,128]{2,1,0:T(8,128)S(1)} %get-tuple-element.22.b, f32[6,64,128]{2,1,0:T(8,128)S(1)} %get-tuple-element.23.inner, f32[9,64,128]{2,1,0:T(8,128)S(1)} %collective-permute-done.5.xa, ...), custom_call_target="tpu_custom_call" | custom-call | flops 4194304 | bytes 1048576 | tf_op jit(solution)/shard_map/pallas_call | solution.py:338
  56.4 1.0 %collective-permute-done.9.yb = f32[64,128]{1,0:T(8,128)S(1)} collective-permute-done((f32[64,128]{1,0:T(8,128)S(1)}, f32[64,128]{1,0:T(8,128)S(1)}, u32[]{:S(2)}, u32[]{:S(2)}) %collective-permute-start.9) | collective-permute-done | bytes 32800 | tf_op jit(solution)/shard_map/ppermute | solution.py:364
  57.3 2.3 %shard_map.36.change = f32[6,4,64,128]{3,2,1,0:T(8,128)S(1)} custom-call(f32[6,4,64,128]{3,2,1,0:T(8,128)S(1)} %shard_map.34.change, f32[9,64,128]{2,1,0:T(8,128)S(1)} %get-tuple-element.21.a, f32[9,64,128]{2,1,0:T(8,128)S(1)} %get-tuple-element.22.b, f32[6,64,128]{2,1,0:T(8,128)S(1)} %get-tuple-element.23.inner, f32[64,128]{1,0:T(8,128)S(1)} %collective-permute-done.8.ya, ...), custom_call_target="tpu_custom_call" | custom-call | flops 2097152 | bytes 1048576 | tf_op jit(solution)/shard_map/pallas_call | solution.py:338
  59.6 3.0 %all-to-all-done.1 = f32[128,1,128]{2,1,0:T(1,128)S(1)} async-done(((f32[128,1,128]{2,1,0:T(1,128)}), f32[128,1,128]{2,1,0:T(1,128)S(1)}, u32[]{:S(2)}, u32[]{:S(2)}) %all-to-all-start.1) | async-done | bytes 65568 | tf_op jit(solution)/shard_map/all_to_all | solution.py:368
  62.6 1.1 %shard_map.38 = f32[6,4,64,128]{3,2,1,0:T(8,128)} custom-call(f32[6,4,64,128]{3,2,1,0:T(8,128)S(1)} %shard_map.36.change, f32[6,4,64,128]{3,2,1,0:T(8,128)S(1)} %get-tuple-element.25.base, f32[128,128]{1,0:T(8,128)S(1)} %bitcast.9), custom_call_target="tpu_custom_call" | custom-call | flops 1 | bytes 1048576 | tf_op jit(solution)/shard_map/pallas_call | solution.py:338
  (11 shorter events, 2.1 us)
Async XLA Ops:
  1.4 25.3 %collective-permute-start = (f32[9,64,128]{2,1,0:T(8,128)S(1)}, f32[9,64,128]{2,1,0:T(8,128)S(1)}, u32[]{:S(2)}, u32[]{:S(2)}) collective-permute-start(f32[9,64,128]{2,1,0:T(8,128)S(1)} %get-tuple-element.16.a), channel_id=1, source_target_pairs={{0,8},{16,24},{32,40},{48,56},{64,72},{80,88},{96,104},{112,120},{... | collective-permute-start | bytes 884744 | tf_op jit(solution)/shard_map/ppermute | solution.py:360
  3.6 23.1 %collective-permute-start.1 = (f32[9,64,128]{2,1,0:T(8,128)S(1)}, f32[9,64,128]{2,1,0:T(8,128)S(1)}, u32[]{:S(2)}, u32[]{:S(2)}) collective-permute-start(f32[9,64,128]{2,1,0:T(8,128)S(1)} %get-tuple-element.17.b), channel_id=1, source_target_pairs={{8,16},{24,32},{40,48},{56,64},{72,80},{88,96},{104,112},{120,128}... | collective-permute-start | bytes 884744 | tf_op jit(solution)/shard_map/ppermute | solution.py:361
  10.8 4.7 %collective-permute-start.2 = (f32[80,128]{1,0:T(8,128)S(1)}, f32[80,128]{1,0:T(8,128)S(1)}, u32[]{:S(2)}, u32[]{:S(2)}) collective-permute-start(f32[80,128]{1,0:T(8,128)S(1)} %get-tuple-element.19), channel_id=1, source_target_pairs={{0,1},{1,0},{2,3},{3,2},{4,5},{5,4},{6,7},{7,6},{8,9},{9,8},{10,11... | collective-permute-start | bytes 122888 | tf_op jit(solution)/shard_map/ppermute | solution.py:362
  16.1 18.7 %all-to-all-start = ((f32[128,1,128]{2,1,0:T(1,128)}), f32[128,1,128]{2,1,0:T(1,128)S(1)}, u32[]{:S(2)}, u32[]{:S(2)}) async-start(f32[128,1,128]{2,1,0:T(1,128)} %bitcast.1), calls=%async_computation | async-start | bytes 131072 | tf_op jit(solution)/shard_map/all_to_all | solution.py:368
  24.8 3.7 %collective-permute-start.3 = (f32[64,128]{1,0:T(8,128)S(1)}, f32[64,128]{1,0:T(8,128)S(1)}, u32[]{:S(2)}, u32[]{:S(2)}) collective-permute-start(f32[64,128]{1,0:T(8,128)S(1)} %shard_map.30), channel_id=1, source_target_pairs={{0,2},{4,6},{2,0},{6,4},{1,3},{5,7},{3,1},{7,5},{8,10},{12,14},{10... | collective-permute-start | bytes 98312 | tf_op jit(solution)/shard_map/ppermute | solution.py:363
  25.8 3.7 %collective-permute-start.4 = (f32[64,128]{1,0:T(8,128)S(1)}, f32[64,128]{1,0:T(8,128)S(1)}, u32[]{:S(2)}, u32[]{:S(2)}) collective-permute-start(f32[64,128]{1,0:T(8,128)S(1)} %shard_map.30), channel_id=1, source_target_pairs={{2,4},{6,0},{4,2},{0,6},{3,5},{7,1},{5,3},{1,7},{10,12},{14,8},{12... | collective-permute-start | bytes 98312 | tf_op jit(solution)/shard_map/ppermute | solution.py:364
  36.2 18.3 %collective-permute-start.5 = (f32[9,64,128]{2,1,0:T(8,128)S(1)}, f32[9,64,128]{2,1,0:T(8,128)S(1)}, u32[]{:S(2)}, u32[]{:S(2)}) collective-permute-start(f32[9,64,128]{2,1,0:T(8,128)S(1)} %get-tuple-element.21.a), channel_id=1, source_target_pairs={{0,8},{16,24},{32,40},{48,56},{64,72},{80,88},{96,104},{112,120},{... | collective-permute-start | bytes 884744 | tf_op jit(solution)/shard_map/ppermute | solution.py:360
  36.5 18.1 %collective-permute-start.6 = (f32[9,64,128]{2,1,0:T(8,128)S(1)}, f32[9,64,128]{2,1,0:T(8,128)S(1)}, u32[]{:S(2)}, u32[]{:S(2)}) collective-permute-start(f32[9,64,128]{2,1,0:T(8,128)S(1)} %get-tuple-element.22.b), channel_id=1, source_target_pairs={{8,16},{24,32},{40,48},{56,64},{72,80},{88,96},{104,112},{120,128}... | collective-permute-start | bytes 884744 | tf_op jit(solution)/shard_map/ppermute | solution.py:361
  38.8 4.4 %collective-permute-start.7 = (f32[80,128]{1,0:T(8,128)S(1)}, f32[80,128]{1,0:T(8,128)S(1)}, u32[]{:S(2)}, u32[]{:S(2)}) collective-permute-start(f32[80,128]{1,0:T(8,128)S(1)} %get-tuple-element.24), channel_id=1, source_target_pairs={{0,1},{1,0},{2,3},{3,2},{4,5},{5,4},{6,7},{7,6},{8,9},{9,8},{10,11... | collective-permute-start | bytes 122888 | tf_op jit(solution)/shard_map/ppermute | solution.py:362
  43.8 18.8 %all-to-all-start.1 = ((f32[128,1,128]{2,1,0:T(1,128)}), f32[128,1,128]{2,1,0:T(1,128)S(1)}, u32[]{:S(2)}, u32[]{:S(2)}) async-start(f32[128,1,128]{2,1,0:T(1,128)} %bitcast.4), calls=%async_computation.1 | async-start | bytes 131072 | tf_op jit(solution)/shard_map/all_to_all | solution.py:368
  52.7 3.7 %collective-permute-start.8 = (f32[64,128]{1,0:T(8,128)S(1)}, f32[64,128]{1,0:T(8,128)S(1)}, u32[]{:S(2)}, u32[]{:S(2)}) collective-permute-start(f32[64,128]{1,0:T(8,128)S(1)} %shard_map.35), channel_id=1, source_target_pairs={{0,2},{4,6},{2,0},{6,4},{1,3},{5,7},{3,1},{7,5},{8,10},{12,14},{10... | collective-permute-start | bytes 98312 | tf_op jit(solution)/shard_map/ppermute | solution.py:363
  53.7 3.7 %collective-permute-start.9 = (f32[64,128]{1,0:T(8,128)S(1)}, f32[64,128]{1,0:T(8,128)S(1)}, u32[]{:S(2)}, u32[]{:S(2)}) collective-permute-start(f32[64,128]{1,0:T(8,128)S(1)} %shard_map.35), channel_id=1, source_target_pairs={{2,4},{6,0},{4,2},{0,6},{3,5},{7,1},{5,3},{1,7},{10,12},{14,8},{12... | collective-permute-start | bytes 98312 | tf_op jit(solution)/shard_map/ppermute | solution.py:364
